TPU v7x, 128 devices: a whole 4x4x4 slice. The times are simulated.
128 devices in a mesh: lon: 16 (over x_lo, z, core), lat: 8 (over y, x_hi).
Axes of the slice: x: 4 (x_hi: 2, x_lo: 2; x = x_hi * 2 + x_lo), y: 4, z: 4, core: 2. Of those that a mesh axis runs over, the one named last changes fastest.
Arguments:
- height: float32 [1, 1152, 4096], P(None, 'lat', 'lon'), may hold values from -6 to 6
- response: float32 [640], replicated, may hold values from 0.25 to 4
Outputs:
- loading: float32 [1, 1152, 4096], P(None, 'lat', 'lon')
All inputs are finite; a program needn't handle non-finite values.
Results may differ from a plain program's by a relative error of at most 0.00085.
Values sent between devices are 32-bit elements; how exact they have to be, the bound alone decides.
A program may use at most 64 MiB of HBM per device.

v0:
```python
import jax
import jax.numpy as jnp
from jax import lax
from jax.sharding import PartitionSpec as P

NLAT = 1152
NLON = 4096
MODES = 640


block_degrees = 64
rescale_every = 8
highest = lax.Precision.HIGHEST


def in_blocks(x, dim, devices):
    shape = x.shape
    blocks = x.reshape(*shape[:dim], devices, shape[dim] // devices, *shape[dim + 1 :])
    return jnp.moveaxis(blocks, dim, 0)


def sent_and_summed(x, axis, dim):
    blocks = in_blocks(x, dim, lax.axis_size(axis))
    arrived = lax.all_to_all(blocks, axis, split_axis=0, concat_axis=0, tiled=True)
    return arrived.sum(axis=0)


def copy_for_each(x, axis):
    copies = jnp.broadcast_to(x, (lax.axis_size(axis), *x.shape))
    return lax.all_to_all(copies, axis, split_axis=0, concat_axis=0, tiled=True)


def laid_out(blocks, dim):
    blocks = jnp.moveaxis(blocks, 0, dim)
    shape = blocks.shape
    return blocks.reshape(*shape[:dim], shape[dim] * shape[dim + 1], *shape[dim + 2 :])


def gathered_copies(x, axis, dim):
    blocks = copy_for_each(x, axis)
    return laid_out(blocks, dim)


def colatitude_parts(latitudes):
    colatitude = (latitudes.astype(jnp.float32) + 0.5) * (jnp.pi / NLAT)
    sines = jnp.sin(colatitude)
    return (jnp.cos(colatitude), sines, sines * (jnp.pi / NLAT))


def legendre_sweep(cosines, sines, orders, consume, initial):
    order_float = orders.astype(jnp.float32)
    log_start = 0.5 * (
        lax.lgamma(order_float + 1.5)
        - lax.lgamma(order_float + 1.0)
        - lax.lgamma(jnp.full_like(order_float, 1.5))
    ) - 0.5 * jnp.log(4.0 * jnp.pi)
    log_scale = log_start[:, None] + order_float[:, None] * jnp.log(sines)[None, :]
    zero_field = jnp.zeros(log_scale.shape, jnp.float32)

    def one_block(block_index, carried):
        earlier, latest, log_scale, running = carried
        first_degree = (block_index * block_degrees).astype(jnp.int32)
        factor = jnp.exp(log_scale)
        layers = []
        for offset in range(block_degrees):
            degree = first_degree + offset
            started = degree > orders
            starting = degree == orders
            degree_float = degree.astype(jnp.float32)
            lower_float = degree_float - 1.0
            square_gap = jnp.where(
                started, degree_float * degree_float - order_float * order_float, 1.0
            )
            growth = jnp.sqrt(
                jnp.where(started, (4.0 * degree_float * degree_float - 1.0) / square_gap, 0.0)
            )
            damping = jnp.sqrt(
                jnp.where(
                    started,
                    (lower_float * lower_float - order_float * order_float)
                    / jnp.maximum(4.0 * lower_float * lower_float - 1.0, 1.0),
                    0.0,
                )
            )
            current = jnp.where(
                starting[:, None],
                1.0,
                growth[:, None] * (cosines[None, :] * latest - damping[:, None] * earlier),
            )
            layers.append(current * factor)
            earlier, latest = (latest, current)
            if (offset + 1) % rescale_every == 0:
                largest = jnp.maximum(jnp.maximum(jnp.abs(earlier), jnp.abs(latest)), 1.0)
                earlier = earlier / largest
                latest = latest / largest
                log_scale = log_scale + jnp.log(largest)
                factor = jnp.exp(log_scale)
        legendre = jnp.stack(layers)
        return (earlier, latest, log_scale, consume(running, legendre, first_degree))

    carried = (zero_field, zero_field, log_scale, initial)
    carried = lax.fori_loop(0, MODES // block_degrees, one_block, carried)
    return carried[3]


def analyse(spectrum, latitudes, orders):
    cosines, sines, weights = colatitude_parts(latitudes)
    weighted = spectrum * weights

    def consume(coefficients, legendre, first_degree):
        block_terms = jnp.einsum("lmj,mcfj->lmcf", legendre, weighted, precision=highest)
        return lax.dynamic_update_slice_in_dim(coefficients, block_terms, first_degree, 0)

    initial = jnp.zeros((MODES,) + spectrum.shape[:3], jnp.float32)
    return legendre_sweep(cosines, sines, orders, consume, initial)


def synthesise(scaled, latitudes, orders):
    cosines, sines = colatitude_parts(latitudes)[:2]

    def consume(running, legendre, first_degree):
        scaled_block = lax.dynamic_slice_in_dim(scaled, first_degree, block_degrees, 0)
        return running + jnp.einsum("lmj,lmcf->mcfj", legendre, scaled_block, precision=highest)

    initial = jnp.zeros(scaled.shape[1:] + (latitudes.shape[0],), jnp.float32)
    return legendre_sweep(cosines, sines, orders, consume, initial)


def angle_table(wavenumbers, longitudes):
    product = wavenumbers[:, None] * longitudes[None, :] % NLON
    return product.astype(jnp.float32) * (2.0 * jnp.pi / NLON)


def forward_terms(field, wavenumbers, longitudes):
    angles = angle_table(wavenumbers, longitudes)
    spacing = 2.0 * jnp.pi / NLON
    real_part = jnp.einsum("mk,fjk->mfj", jnp.cos(angles) * spacing, field, precision=highest)
    imag_part = -jnp.einsum("mk,fjk->mfj", jnp.sin(angles) * spacing, field, precision=highest)
    return jnp.stack([real_part, imag_part], axis=1)


def inverse_terms(spectral_parts, wavenumbers, longitudes):
    angles = angle_table(wavenumbers, longitudes)
    weight = jnp.where(wavenumbers == 0, 1.0, 2.0)[:, None]
    real_part = jnp.einsum(
        "mk,mfj->fjk", jnp.cos(angles) * weight, spectral_parts[:, 0], precision=highest
    )
    imag_part = jnp.einsum(
        "mk,mfj->fjk", jnp.sin(angles) * weight, spectral_parts[:, 1], precision=highest
    )
    return real_part - imag_part


def shards(height, response):
    fields, band_rows, lon_cells = height.shape
    lon_count = lax.axis_size("lon")
    lat_count = lax.axis_size("lat")
    lon_index = lax.axis_index("lon")
    lat_index = lax.axis_index("lat")
    local_modes = MODES // lon_count
    longitudes = lon_index * lon_cells + jnp.arange(lon_cells, dtype=jnp.int32)
    wavenumbers = jnp.arange(local_modes * lax.axis_size("lon"), dtype=jnp.int32)
    spectrum = sent_and_summed(forward_terms(height, wavenumbers, longitudes), "lon", 0)
    column_modes = local_modes // lat_count
    columns = lax.all_to_all(spectrum, "lat", split_axis=0, concat_axis=3, tiled=True)
    all_latitudes = jnp.arange(NLAT, dtype=jnp.int32)
    column_orders = (
        lon_index * local_modes
        + lat_index * column_modes
        + jnp.arange(column_modes, dtype=jnp.int32)
    )
    coefficients = analyse(columns, all_latitudes, column_orders)
    scaled = coefficients * response[:, None, None, None]
    column_synthesis = synthesise(scaled, all_latitudes, column_orders)
    synthesis = lax.all_to_all(column_synthesis, "lat", split_axis=3, concat_axis=0, tiled=True)
    shard_piece = gathered_copies(synthesis, "lon", 0)
    wavenumbers = jnp.arange(shard_piece.shape[0], dtype=jnp.int32)
    return inverse_terms(shard_piece, wavenumbers, longitudes)


def solution(mesh):
    placed = (P(None, "lat", "lon"), P())
    return jax.shard_map(
        shards, mesh=mesh, in_specs=placed, out_specs=P(None, "lat", "lon"), check_vma=False
    )
```

profile of v0, /device:TPU:1, one launch (start us, length us, event | category | flops | bytes accessed | tf_op | source)
XLA Modules:
  0.0 324.2 jit_solution(3746720195332624760)
XLA Ops:
  0.9 3.2 convolution_negate_fusion
  4.3 3.1 convolution_bitcast_fusion.2
  8.8 7.7 %all-to-all-start = ((f32[16,40,2,1,144]{4,1,3,2,0:T(8,128)}), f32[16,40,2,1,144]{4,1,3,2,0:T(8,128)S(1)}, u32[]{:S(2)}, u32[]{:S(2)}) async-start(f32[16,40,2,1,144]{4,1,3,2,0:T(8,128)} %copy.655), calls=%async_computation | async-start | bytes 2621440 | tf_op jit(solution)/shard_map/all_to_all | solution.py:24
  16.8 18.3 %all-to-all-done = f32[16,40,2,1,144]{4,1,3,2,0:T(8,128)S(1)} async-done(((f32[16,40,2,1,144]{4,1,3,2,0:T(8,128)}), f32[16,40,2,1,144]{4,1,3,2,0:T(8,128)S(1)}, u32[]{:S(2)}, u32[]{:S(2)}) %all-to-all-start) | async-done | bytes 737312 | tf_op jit(solution)/shard_map/all_to_all | solution.py:24
  35.8 6.6 %all-to-all-start.1 = ((f32[40,2,1,144]{3,1,2,0:T(2,128)}), f32[40,2,1,144]{3,1,2,0:T(2,128)S(1)}, u32[]{:S(2)}, u32[]{:S(2)}) async-start(f32[40,2,1,144]{3,1,2,0:T(2,128)} %copy.657), calls=%async_computation.1 | async-start | bytes 163840 | tf_op jit(solution)/shard_map/all_to_all | solution.py:165
  42.5 6.6 %all-to-all-done.1 = f32[40,2,1,144]{3,1,2,0:T(2,128)S(1)} async-done(((f32[40,2,1,144]{3,1,2,0:T(2,128)}), f32[40,2,1,144]{3,1,2,0:T(2,128)S(1)}, u32[]{:S(2)}, u32[]{:S(2)}) %all-to-all-start.1) | async-done | bytes 46112 | tf_op jit(solution)/shard_map/all_to_all | solution.py:165
  49.3 117.3 %while.52 = (s32[]{:T(128)}, f32[5,1152]{1,0:T(8,128)S(1)}, f32[5,1152]{1,0:T(8,128)S(1)}, f32[5,1152]{1,0:T(8,128)S(1)}, f32[640,5,2,1]{0,2,1,3:T(2,128)S(1)}, ...) while((s32[]{:T(128)}, f32[5,1152]{1,0:T(8,128)S(1)}, ...), condition=%wide.region_2.3_spmd.clone.clone.clone.clone, body=%wide.region_1.2_spmd.clone.clone.clone.clone.sunk | while | flops 11932070 | bytes 11638224 | solution.py:102
  52.4 1.5 exponential_multiply_fusion.4
  56.8 2.3 stack.1964
  59.1 1.4 convolution_bitcast_fusion.4
  63.8 1.5 exponential_multiply_fusion.4
  68.2 2.3 stack.1964
  70.5 1.4 convolution_bitcast_fusion.4
  75.8 1.5 exponential_multiply_fusion.4
  80.3 2.3 stack.1964
  82.6 1.4 convolution_bitcast_fusion.4
  87.2 1.5 exponential_multiply_fusion.4
  91.7 2.3 stack.1964
  94.0 1.4 convolution_bitcast_fusion.4
  99.3 1.5 exponential_multiply_fusion.4
  103.8 2.3 stack.1964
  106.0 1.4 convolution_bitcast_fusion.4
  110.7 1.5 exponential_multiply_fusion.4
  115.2 2.3 stack.1964
  117.4 1.4 convolution_bitcast_fusion.4
  122.8 1.5 exponential_multiply_fusion.4
  127.2 2.3 stack.1964
  129.5 1.4 convolution_bitcast_fusion.4
  134.2 1.5 exponential_multiply_fusion.4
  138.6 2.3 stack.1964
  140.9 1.4 convolution_bitcast_fusion.4
  146.3 1.5 exponential_multiply_fusion.4
  150.7 2.3 stack.1964
  153.0 1.4 convolution_bitcast_fusion.4
  157.6 1.5 exponential_multiply_fusion.4
  162.1 2.3 stack.1964
  166.7 106.4 %while.53 = (s32[]{:T(128)}, f32[5,1152]{1,0:T(8,128)S(1)}, f32[5,1152]{1,0:T(8,128)S(1)}, f32[5,1152]{1,0:T(8,128)S(1)}, f32[5,2,1,1152]{3,1,0,2:T(2,128)S(1)},...) while((s32[]{:T(128)}, f32[5,1152]{1,0:T(8,128)S(1)}, ...), condition=%wide.region_4.5_spmd.clone.clone.clone.clone, body=%wide.region_3.4_spmd.clone.clone.clone.clone.sunk | while | flops 11955110 | bytes 11681745 | solution.py:102
  169.9 1.5 exponential_multiply_fusion.5
  174.4 2.3 stack.1966
  180.6 1.5 exponential_multiply_fusion.5
  185.0 2.3 stack.1966
  191.2 1.5 exponential_multiply_fusion.5
  195.6 2.3 stack.1966
  201.8 1.5 exponential_multiply_fusion.5
  206.3 2.3 stack.1966
  212.4 1.5 exponential_multiply_fusion.5
  216.9 2.3 stack.1966
  223.1 1.5 exponential_multiply_fusion.5
  227.5 2.3 stack.1966
  233.7 1.5 exponential_multiply_fusion.5
  238.1 2.3 stack.1966
  244.3 1.5 exponential_multiply_fusion.5
  248.7 2.3 stack.1966
  254.9 1.5 exponential_multiply_fusion.5
  259.4 2.3 stack.1966
  265.5 1.5 exponential_multiply_fusion.5
  270.0 2.3 stack.1966
  274.3 1.6 reshape.6694
  275.9 9.3 %all_to_all.46 = f32[8,1,1440]{2,1,0:T(1,128)S(1)} all-to-all(f32[8,1,1440]{2,1,0:T(1,128)S(1)} %reshape.6694), channel_id=1, replica_groups=mesh['lon'=16,'lat'=8] {'lat'}, dimensions={0} | all-to-all | bytes 92160 | tf_op jit(solution)/shard_map/all_to_all | solution.py:175
  286.5 1.7 reshape.6695
  290.2 7.1 %all-to-all-start.3 = ((f32[16,40,2,1,144]{4,1,2,3,0:T(8,128)}), f32[16,40,2,1,144]{4,1,2,3,0:T(8,128)S(1)}, u32[]{:S(2)}, u32[]{:S(2)}) async-start(f32[16,40,2,1,144]{4,1,2,3,0:T(8,128)} %broadcast_in_dim.4429), calls=%async_computation.3 | async-start | bytes 2621440 | tf_op jit(solution)/shard_map/all_to_all | solution.py:30
  297.3 18.6 %all-to-all-done.3 = f32[16,40,2,1,144]{4,1,2,3,0:T(8,128)S(1)} async-done(((f32[16,40,2,1,144]{4,1,2,3,0:T(8,128)}), f32[16,40,2,1,144]{4,1,2,3,0:T(8,128)S(1)}, u32[]{:S(2)}, u32[]{:S(2)}) %all-to-all-start.3) | async-done | bytes 737312 | tf_op jit(solution)/shard_map/all_to_all | solution.py:30
  316.0 3.6 %fusion.435 = f32[144,256]{1,0:T(8,128)S(1)} fusion(f32[640,2,1,144]{3,0,1,2:T(8,128)S(1)} %bitcast.1891, f32[640]{0:T(1024)S(1)} %fusion.463, s32[256]{0:T(256)S(1)} %iota_add_fusion.2), kind=kOutput, calls=%fused_computation.1122 | convolution fusion | flops 285573120 | bytes 807936 | tf_op jit(solution)/shard_map/mk,mfj->fjk/dot_general | solution.py:145
  319.5 4.3 %fusion.425 = f32[1,144,256]{2,1,0:T(8,128)} fusion(f32[144,256]{1,0:T(8,128)S(1)} %fusion.435, f32[640,2,1,144]{3,0,1,2:T(8,128)S(1)} %bitcast.1892, f32[640]{0:T(1024)S(1)} %fusion.463, s32[256]{0:T(256)S(1)} %iota_add_fusion.2), kind=kOutput, calls=%fused_computation.1106 | convolution fusion | flops 285609984 | bytes 955392 | tf_op jit(solution)/shard_map/mk,mfj->fjk/dot_general | solution.py:148
  (3456 shorter events, 98.8 us)
Async XLA Ops:
  0.0 0.9 copy-start
  8.8 26.3 %all-to-all-start = ((f32[16,40,2,1,144]{4,1,3,2,0:T(8,128)}), f32[16,40,2,1,144]{4,1,3,2,0:T(8,128)S(1)}, u32[]{:S(2)}, u32[]{:S(2)}) async-start(f32[16,40,2,1,144]{4,1,3,2,0:T(8,128)} %copy.655), calls=%async_computation | async-start | bytes 2621440 | tf_op jit(solution)/shard_map/all_to_all | solution.py:24
  35.8 13.3 %all-to-all-start.1 = ((f32[40,2,1,144]{3,1,2,0:T(2,128)}), f32[40,2,1,144]{3,1,2,0:T(2,128)S(1)}, u32[]{:S(2)}, u32[]{:S(2)}) async-start(f32[40,2,1,144]{3,1,2,0:T(2,128)} %copy.657), calls=%async_computation.1 | async-start | bytes 163840 | tf_op jit(solution)/shard_map/all_to_all | solution.py:165
  49.3 117.4 %copy-start.1 = (f32[640]{0:T(1024)S(1)}, f32[640]{0:T(1024)}, u32[]{:S(2)}) copy-start(f32[640]{0:T(1024)} %param.7) | copy-start | bytes 7684
  290.2 25.7 %all-to-all-start.3 = ((f32[16,40,2,1,144]{4,1,2,3,0:T(8,128)}), f32[16,40,2,1,144]{4,1,2,3,0:T(8,128)S(1)}, u32[]{:S(2)}, u32[]{:S(2)}) async-start(f32[16,40,2,1,144]{4,1,2,3,0:T(8,128)} %broadcast_in_dim.4429), calls=%async_computation.3 | async-start | bytes 2621440 | tf_op jit(solution)/shard_map/all_to_all | solution.py:30
where the time goes:
time: 330 us; the launch traced here: 324 us
  local copies, waits for them, and re-layouts  92.9 us (28%)
  other arithmetic  75.1 us (23%)
  loops' own time  44.1 us (13%)
  waiting for transfers between devices  43.5 us (13%)
  matrix products  37.4 us (11%)
  starting transfers between devices  21.4 us (6%)
  blocking collectives  9.27 us (3%)
    another operation x1300, local copies, waits for them, and re-layouts, one_block(): legendre = jnp.stack(layers)  77.4 us
    another operation x2, loops' own time, legendre_sweep(): carried = lax.fori_loop(0, MODES // block_degrees, one_block, carried)  44.1 us
    mul x20, other arithmetic, one_block(): layers.append(current * factor)  30.9 us
    all_to_all x1, waiting for transfers between devices, copy_for_each(): return lax.all_to_all(copies, axis, split_axis=0, concat_axis=0, tiled=True)  18.6 us
    all_to_all x1, waiting for transfers between devices, sent_and_summed(): lax.all_to_all(blocks, axis, split_axis=0, concat_axis=0, tiled=True)  18.3 us
    another operation x180, other arithmetic, one_block(): legendre = jnp.stack(layers)  15.1 us
    dot_general x10, matrix products, consume(): jnp.einsum('lmj,mcfj->lmcf', legendre, weighted, precision=highest)  14.5 us
    sqrt x640, other arithmetic, one_block(): jnp.sqrt(jnp.where(started, (4.0 * degree_float * degree_float - 1.0) / s...  11.8 us
  transfers between devices with their start and end apart: 3, of which 3 were waited for; matrix products, arithmetic and copies ran while one was open for 0% of the time, Pallas kernels for 0%

commit v1 on v0

v1 whole, which is shorter than its diff:
```python
import math

import jax
import jax.numpy as jnp
import numpy as np
from jax import lax
from jax.experimental import pallas as pl
from jax.experimental.pallas import tpu as pltpu
from jax.sharding import PartitionSpec as P

NLAT = 1152
NLON = 4096
MODES = 640
LON = 16
LAT = 8
DEV = LON * LAT
ROWS = NLAT // DEV
CELLS = NLON // LON
SLOTS = MODES // DEV
HALF = DEV // 2
STARTS = [sum(MODES - DEV * t for t in range(i)) for i in range(SLOTS)]
TALL = sum(MODES - DEV * t for t in range(SLOTS))
WIDE = 640
bf16 = jnp.bfloat16
f32 = jnp.float32


def constants():
    t = np.arange(CELLS)
    table = np.zeros((2 * CELLS, 128))
    for g in range(LAT):
        for i in range(SLOTS):
            angle = 2 * np.pi * ((g + LAT * i) * t % CELLS) / CELLS
            column = (g * SLOTS + i) * 2
            table[:CELLS, column] = np.cos(angle)
            table[CELLS:, column] = np.sin(angle)
            table[:CELLS, column + 1] = -np.sin(angle)
            table[CELLS:, column + 1] = np.cos(angle)
    high = table.astype(np.float32).astype(bf16)
    low = (table - high.astype(np.float64)).astype(np.float32).astype(bf16)
    angle = 2 * np.pi * np.arange(LON)[:, None] * t[None, :] / NLON
    twiddle = np.stack([np.cos(angle), np.sin(angle)]).astype(np.float32)
    geometry = np.zeros((4, 8, 128), np.float32)
    for chunk in range(5):
        for lane in range(128):
            r = 2 * chunk + lane // HALF
            if r < ROWS:
                theta = np.pi * (ROWS * (lane % HALF) + r + 0.5) / NLAT
                log_sine = np.log2(np.sin(theta))
                coarse = np.round(log_sine * 1024) / 1024
                geometry[:, chunk, lane] = np.cos(theta), coarse, log_sine - coarse, 1.0
    weights = np.zeros((HALF, 128), np.float32)
    for r in range(ROWS):
        theta = np.pi * (ROWS * np.arange(HALF) + r + 0.5) / NLAT
        cell = np.sin(theta) * (np.pi / NLAT) * (2 * np.pi / NLON)
        weights[:, 10 * r : 10 * r + 10] = cell[:, None]
    first = [
        (0.5 * (math.lgamma(m + 1.5) - math.lgamma(1.5) - math.lgamma(m + 1.0)) - 0.5 * math.log(4 * math.pi))
        / math.log(2)
        for m in range(MODES)
    ]
    return high, low, twiddle, geometry, weights, np.asarray(first, np.float32)


def split(x):
    high = x.astype(bf16)
    return high, (x - high.astype(f32)).astype(bf16)


def cosine(n):
    return math.cos(math.pi * (n % 16) / 8)


def sine(n):
    return math.sin(math.pi * (n % 16) / 8)


def combine(terms):
    total = None
    for value, factor in terms:
        if abs(factor) < 1e-9:
            continue
        if abs(factor - 1) < 1e-9:
            term, negative = value, False
        elif abs(factor + 1) < 1e-9:
            term, negative = value, True
        else:
            term, negative = value * factor, False
        if total is None:
            total = -term if negative else term
        else:
            total = total - term if negative else total + term
    return 0.0 if total is None else total


def kernel(
    h_ref, resp_ref, thi_ref, tlo_ref, tw_ref, geo_ref, wt_ref, lc_ref, o_ref,
    send_a, recv_a, zs, osc, send_b, recv_b, coef_a, coef_c, tall, phi, plo, fold, send_c, recv_c, vs, send_d, recv_d,
    ssem, rsem,
):
    lon = lax.axis_index("lon")
    lat = lax.axis_index("lat")
    me = lat * LON + lon
    south = lat // (LAT // 2)
    barrier = pltpu.get_barrier_semaphore()

    def peer(p):
        return {"lat": p // LON, "lon": p % LON}

    def place(p):
        return jnp.where(p < HALF, p, DEV + HALF - 1 - p)

    def greet(step, carry):
        pl.semaphore_signal(barrier, inc=1, device_id=peer(lax.rem(me + step, DEV)))
        return carry

    lax.fori_loop(1, DEV, greet, 0)

    def stage(block, carry):
        for r in range(ROWS):
            source = jnp.where(south == 1, ROWS - 1 - r, r)
            send_a[block, r : r + 1, :] = h_ref[pl.ds(ROWS * block + source, 1), :]
        return carry

    lax.fori_loop(0, LON, stage, 0)

    for i in range(SLOTS):
        def coefficients(block, carry, i=i):
            row = block * 32
            m = (DEV * i + me).astype(f32)
            k = (row + lax.broadcasted_iota(jnp.int32, (32, 128), 0)).astype(f32)
            k1 = k + 1.0
            l2 = 2.0 * (m + k1)
            squared = (l2 * l2 - 1.0) / (k1 * (2.0 * m + k1))
            below = l2 - 2.0
            ratio = k * (2.0 * m + k) / jnp.maximum(below * below - 1.0, 1.0)
            start = pl.multiple_of(STARTS[i] + row, 8)
            coef_a[pl.ds(start, 32), :] = jnp.sqrt(squared)
            coef_c[pl.ds(start, 32), :] = jnp.sqrt(squared * ratio)
            return carry

        lax.fori_loop(0, (MODES - DEV * i) // 32, coefficients, 0)

    pl.semaphore_wait(barrier, DEV - 1)

    def exchange_lon(send, recv, which):
        def go(step, carry):
            p = lax.rem(lon + step, LON)
            pltpu.make_async_remote_copy(
                send.at[p], recv.at[lon], ssem.at[which], rsem.at[which], device_id={"lat": lat, "lon": p}
            ).start()
            return carry

        lax.fori_loop(1, LON, go, 0)
        recv[lon] = send[lon]

    def finish(send, recv, which, count):
        every = pltpu.make_async_remote_copy(
            send.at[pl.ds(0, count)], recv.at[pl.ds(0, count)], ssem.at[which], rsem.at[which],
            device_id=peer(lax.rem(me + 1, DEV)),
        )
        every.wait_send()
        every.wait_recv()

    exchange_lon(send_a, recv_a, 0)

    x = geo_ref[0]
    state = []
    for i in range(SLOTS):
        m = (DEV * i + me).astype(f32)
        coarse = m * geo_ref[1]
        fine = m * geo_ref[2] + lc_ref[DEV * i + me]
        count = jnp.maximum(jnp.ceil((-84.0 - (coarse + fine)) * (1.0 / 64.0)), 0.0)
        value = jnp.exp2((coarse + 64.0 * count) + fine) * geo_ref[3]
        state.append((jnp.zeros_like(value), value, count))

    for section in range(SLOTS):
        active = SLOTS - section

        def steps(block, carry, section=section, active=active):
            new = []
            for i in range(active):
                earlier, latest, count = carry[i]
                base = STARTS[i] + section * DEV
                row = pl.multiple_of(base + block * 8, 8)
                a8 = coef_a[pl.ds(row, 8), :]
                c8 = coef_c[pl.ds(row, 8), :]
                seen = jnp.where(count == 0.0, 1.0, 0.0)
                for u in range(8):
                    tall[pl.ds(pl.multiple_of((row + u) * 8, 8), 8), :] = latest * seen
                    following = (a8[u : u + 1, :] * x) * latest - c8[u : u + 1, :] * earlier
                    earlier, latest = latest, following
                large = jnp.logical_and(jnp.abs(latest) > 2.0**-20, count > 0.0)
                factor = jnp.where(large, 2.0**-64, 1.0)
                new.append((earlier * factor, latest * factor, count - jnp.where(large, 1.0, 0.0)))
            return tuple(new)

        state = list(lax.fori_loop(0, DEV // 8, steps, tuple(state[:active])))

    def halves(block, carry):
        row = pl.multiple_of(block * 16, 16)
        for j in range(5):
            value = tall[pl.ds(row * 8 + j, 16, stride=8), :]
            high, low = split(value)
            phi[pl.ds(row, 16), j * 128 : (j + 1) * 128] = high
            plo[pl.ds(row, 16), j * 128 : (j + 1) * 128] = low
        return carry

    lax.fori_loop(0, TALL // 16, halves, 0)

    finish(send_a, recv_a, 0, LON - 1)

    for side in range(2):
        lanes = slice(side * 128, side * 128 + 128)
        d = [recv_a[b, :, lanes] for b in range(LON)]
        even = {b: d[b] + d[16 - b] for b in range(1, 8)}
        odd = {b: d[b] - d[16 - b] for b in range(1, 8)}
        real = [None] * 9
        imag = [None] * 9
        for rho in range(5):
            a = combine(
                [(d[0], 1.0), (d[8], 1.0 - 2.0 * (rho % 2))] + [(even[b], cosine(rho * b)) for b in (2, 4, 6)]
            )
            b_ = combine([(even[b], cosine(rho * b)) for b in (1, 3, 5, 7)])
            e = combine([(odd[b], -sine(rho * b)) for b in (2, 4, 6)])
            c = combine([(odd[b], -sine(rho * b)) for b in (1, 3, 5, 7)])
            real[rho], real[8 - rho] = a + b_, a - b_
            imag[rho], imag[8 - rho] = c + e, c - e
        for rho in range(LON):
            tc = tw_ref[0, rho : rho + 1, lanes]
            ts = tw_ref[1, rho : rho + 1, lanes]
            if rho % 8 == 0:
                zre, zim = real[rho] * tc, -(real[rho] * ts)
            elif rho < 8:
                zre, zim = real[rho] * tc + imag[rho] * ts, imag[rho] * tc - real[rho] * ts
            else:
                yre, yim = real[16 - rho], imag[16 - rho]
                zre, zim = yre * tc - yim * ts, -(yim * tc) - yre * ts
            zs[rho, 0:ROWS, lanes] = zre
            zs[rho, 0:ROWS, CELLS + side * 128 : CELLS + side * 128 + 128] = zim

    zh, zl = split(zs[...].reshape(LON * 16, 2 * CELLS))
    thi = thi_ref[...]
    tlo = tlo_ref[...]
    dims = (((1,), (0,)), ((), ()))
    osc[...] = (
        lax.dot_general(zh, thi, dims, preferred_element_type=f32)
        + lax.dot_general(zl, thi, dims, preferred_element_type=f32)
        + lax.dot_general(zh, tlo, dims, preferred_element_type=f32)
    )

    lane = lax.broadcasted_iota(jnp.int32, (LON, 128), 1)
    packed = [jnp.zeros((LON, 128), f32) for _ in range(LAT)]
    for r in range(ROWS):
        value = osc[pl.ds(r, LON, stride=16), :]
        mine = jnp.logical_and(lane >= 10 * r, lane < 10 * r + 10)
        for g in range(LAT):
            shift = (10 * (r - g)) % 128
            moved = pltpu.roll(value, shift, axis=1) if shift else value
            packed[g] = jnp.where(mine, moved, packed[g])
    for g in range(LAT):
        send_b[g * LON : (g + 1) * LON, 0, :] = packed[g]

    def exchange_all(send, recv, which, source, target):
        def go(step, carry):
            p = lax.rem(me + step, DEV)
            pltpu.make_async_remote_copy(
                send.at[source(p)], recv.at[target], ssem.at[which], rsem.at[which], device_id=peer(p)
            ).start()
            return carry

        lax.fori_loop(1, DEV, go, 0)
        recv[target] = send[source(me)]

    exchange_all(send_b, recv_b, 1, lambda p: p, place(me))

    wide = jnp.concatenate([resp_ref[...], jnp.zeros((1, MODES), f32)], axis=1)
    shifted = pltpu.roll(jnp.broadcast_to(wide, (8, 2 * MODES)), lax.rem(2 * MODES - me, 2 * MODES), axis=1)
    response = jnp.concatenate([shifted[:1, DEV * i : MODES] for i in range(SLOTS)], axis=1)
    first = jnp.where(jnp.logical_and(lax.broadcasted_iota(jnp.int32, (1, TALL), 1) < MODES, me == 0), 1.0, 2.0)
    response = response * first
    row = lax.broadcasted_iota(jnp.int32, (32, TALL), 0)
    column = lax.broadcasted_iota(jnp.int32, (32, TALL), 1)
    slot = jnp.zeros((32, TALL), jnp.int32)
    for i in range(1, SLOTS):
        slot = slot + jnp.where(column >= STARTS[i], 1, 0)
    wanted = 2 * slot + 16 * (column & 1)
    keep = jnp.logical_or(row == wanted, row == wanted + 1)
    gain = jnp.where(keep, response, 0.0)

    finish(send_b, recv_b, 1, DEV - 1)

    north = recv_b[0:HALF, 0, :]
    southern = recv_b[HALF:DEV, 0, :]
    weights = wt_ref[...]
    folded = jnp.concatenate([(north + southern) * weights, (north - southern) * weights], axis=0)
    fold[...] = folded.T
    left = lax.broadcasted_iota(jnp.int32, (10, 128), 1) < HALF
    evens = []
    odds = []
    for j in range(5):
        first_row = fold[20 * j : 20 * j + 10, :]
        if j < 4:
            second_row = fold[20 * j + 10 : 20 * j + 20, :]
        else:
            second_row = jnp.zeros((10, 128), f32)
        evens.append(jnp.where(left, first_row, pltpu.roll(second_row, HALF, axis=1)))
        odds.append(jnp.where(left, pltpu.roll(first_row, HALF, axis=1), second_row))
    pad = jnp.zeros((6, WIDE), f32)
    lhs = jnp.concatenate([jnp.concatenate(evens, axis=1), pad, jnp.concatenate(odds, axis=1), pad], axis=0)
    lh, ll = split(lhs)
    nt = (((1,), (1,)), ((), ()))
    coefficients_ = (
        lax.dot_general(lh, phi[...], nt, preferred_element_type=f32)
        + lax.dot_general(ll, phi[...], nt, preferred_element_type=f32)
        + lax.dot_general(lh, plo[...], nt, preferred_element_type=f32)
    )
    sh, sl = split(coefficients_ * gain)
    synthesis = (
        lax.dot_general(sh, phi[...], dims, preferred_element_type=f32)
        + lax.dot_general(sl, phi[...], dims, preferred_element_type=f32)
        + lax.dot_general(sh, plo[...], dims, preferred_element_type=f32)
    )
    fold[...] = jnp.zeros((128, 128), f32)
    for j in range(5):
        e = synthesis[0:10, j * 128 : (j + 1) * 128]
        o = synthesis[16:26, j * 128 : (j + 1) * 128]
        n, s = e + o, e - o
        fold[20 * j : 20 * j + 10, :] = jnp.where(left, n, pltpu.roll(s, HALF, axis=1))
        if j < 4:
            fold[20 * j + 10 : 20 * j + 20, :] = jnp.where(left, pltpu.roll(n, HALF, axis=1), s)
    send_c[:, 0, :] = fold[...].T

    exchange_all(send_c, recv_c, 2, place, me)
    finish(send_c, recv_c, 2, DEV - 1)

    pieces = [recv_c[g * LON : (g + 1) * LON, 0, :] for g in range(LAT)]
    gathered = []
    for r in range(ROWS):
        value = jnp.zeros((LON, 128), f32)
        for g in range(LAT):
            mine = jnp.logical_and(lane >= 10 * g, lane < 10 * g + 10)
            shift = (10 * (g - r)) % 128
            moved = pltpu.roll(pieces[g], shift, axis=1) if shift else pieces[g]
            value = jnp.where(mine, moved, value)
        gathered.append(value)
    gh, gl = split(jnp.concatenate(gathered, axis=0))
    inverse = (
        lax.dot_general(gh, thi, nt, preferred_element_type=f32)
        + lax.dot_general(gl, thi, nt, preferred_element_type=f32)
        + lax.dot_general(gh, tlo, nt, preferred_element_type=f32)
    )
    for c in range(4):
        vs[c] = inverse[:, c * 128 : (c + 1) * 128]

    for side in range(2):
        lanes = slice(side * 128, side * 128 + 128)
        real = []
        imag = []
        for rho in range(LON):
            tc = tw_ref[0, rho : rho + 1, lanes]
            ts = tw_ref[1, rho : rho + 1, lanes]
            vre = vs[side, pl.ds(rho, ROWS, stride=16), :]
            vim = vs[2 + side, pl.ds(rho, ROWS, stride=16), :]
            real.append(vre * tc - vim * ts)
            imag.append(None if rho % 8 == 0 else vre * ts + vim * tc)
        ure = {rho: real[rho] + real[16 - rho] for rho in range(1, 8)}
        uim = {rho: imag[rho] - imag[16 - rho] for rho in range(1, 8)}
        for b in range(5):
            ge = combine(
                [(real[0], 1.0), (real[8], 1.0 - 2.0 * (b % 2))] + [(ure[q], cosine(q * b)) for q in (2, 4, 6)]
            )
            go = combine([(ure[q], cosine(q * b)) for q in (1, 3, 5, 7)])
            he = combine([(uim[q], sine(q * b)) for q in (2, 4, 6)])
            ho = combine([(uim[q], sine(q * b)) for q in (1, 3, 5, 7)])
            send_d[b, :, lanes] = (ge + go) - (he + ho)
            if b > 0:
                send_d[16 - b, :, lanes] = (ge + go) + (he + ho)
            if b < 4:
                send_d[8 - b, :, lanes] = (ge - go) - (ho - he)
                if b > 0:
                    send_d[8 + b, :, lanes] = (ge - go) + (ho - he)

    exchange_lon(send_d, recv_d, 3)
    finish(send_d, recv_d, 3, LON - 1)

    def unstage(block, carry):
        for r in range(ROWS):
            target = jnp.where(south == 1, ROWS - 1 - r, r)
            o_ref[pl.ds(ROWS * block + target, 1), :] = recv_d[block, r : r + 1, :]
        return carry

    lax.fori_loop(0, LON, unstage, 0)


def shards(height, response):
    high, low, twiddle, geometry, weights, first = constants()
    vmem = pl.BlockSpec(memory_space=pltpu.VMEM)
    smem = pl.BlockSpec(memory_space=pltpu.SMEM)
    blocks = pltpu.VMEM((LON, ROWS, CELLS), f32)
    rows = pltpu.VMEM((DEV, 1, 128), f32)
    out = pl.pallas_call(
        kernel,
        out_shape=jax.ShapeDtypeStruct((NLAT // LAT, CELLS), f32),
        in_specs=[vmem] * 7 + [smem],
        out_specs=vmem,
        scratch_shapes=[
            blocks,
            blocks,
            pltpu.VMEM((LON, 16, 2 * CELLS), f32),
            pltpu.VMEM((LON * 16, 128), f32),
            rows,
            rows,
            pltpu.VMEM((TALL, 128), f32),
            pltpu.VMEM((TALL, 128), f32),
            pltpu.VMEM((TALL * 8, 128), f32),
            pltpu.VMEM((TALL, WIDE), bf16),
            pltpu.VMEM((TALL, WIDE), bf16),
            pltpu.VMEM((128, 128), f32),
            rows,
            rows,
            pltpu.VMEM((4, ROWS * LON, 128), f32),
            blocks,
            blocks,
            pltpu.SemaphoreType.DMA((4,)),
            pltpu.SemaphoreType.DMA((4,)),
        ],
        compiler_params=pltpu.CompilerParams(
            collective_id=0, has_side_effects=True, vmem_limit_bytes=60 * 1024 * 1024
        ),
    )(
        height.reshape(NLAT // LAT, CELLS),
        response.reshape(1, MODES),
        jnp.asarray(high),
        jnp.asarray(low),
        jnp.asarray(twiddle),
        jnp.asarray(geometry),
        jnp.asarray(weights),
        jnp.asarray(first),
    )
    return out.reshape(height.shape)


def solution(mesh):
    placed = (P(None, "lat", "lon"), P())
    return jax.shard_map(
        shards, mesh=mesh, in_specs=placed, out_specs=P(None, "lat", "lon"), check_vma=False
    )
```

time: 330 us -> 46.7 us (0.14); the launches traced: 324 us -> 46.5 us
  local copies, waits for them, and re-layouts: 92.9 us -> 2.85 us
  other arithmetic: 75.1 us -> 0 us
  loops' own time: 44.1 us -> 0 us
  Pallas kernels: 0 us -> 43.6 us
  waiting for transfers between devices: 43.5 us -> 0 us
  matrix products: 37.4 us -> 0 us
  starting transfers between devices: 21.4 us -> 0 us
  blocking collectives: 9.27 us -> 0 us
    another operation x1301 -> x0, local copies, waits for them, and re-layouts: 78.6 us -> none  [the longest x1300 77.4 us: one_block(): legendre = jnp.stack(layers)]
    another operation x2 -> x0, loops' own time: 44.1 us -> none  [legendre_sweep(): carried = lax.fori_loop(0, MODES // block_degrees, one_block, carried)]
    pallas_call x0 -> x1, Pallas kernels: none -> 43.6 us  [shards(): pl.pallas_call(kernel, out_shape=jax.ShapeDtypeStruct((NLAT // LAT, CELLS...]
    all_to_all x3 -> x0, waiting for transfers between devices: 43.5 us -> none  [the longest x1 18.6 us: copy_for_each(): return lax.all_to_all(copies, axis, split_axis=0, concat_axis=0, tiled=True)]
    dot_general x24 -> x0, matrix products: 37.4 us -> none  [the longest x10 14.5 us: consume(): jnp.einsum('lmj,mcfj->lmcf', legendre, weighted, precision=highest)]
    mul x24 -> x0, other arithmetic: 31 us -> none  [the longest x20 30.9 us: one_block(): layers.append(current * factor)]
    sqrt x1280 -> x0, other arithmetic: 21.6 us -> none  [the longest x640 11.8 us: one_block(): jnp.sqrt(jnp.where(started, (4.0 * degree_float * degree_float - 1.0) / s...]
    all_to_all x3 -> x0, starting transfers between devices: 21.4 us -> none  [the longest x1 7.74 us: sent_and_summed(): lax.all_to_all(blocks, axis, split_axis=0, concat_axis=0, tiled=True)]
  transfers between devices with their start and end apart: 3 -> 0, of which waited for: 3 -> 0; matrix products, arithmetic and copies ran while one was open for 0% -> 0% of each run, Pallas kernels for 0% -> 0%
where the time goes in v1:
time: 46.7 us; the launch traced here: 46.5 us
  Pallas kernels  43.6 us (93%)
  local copies, waits for them, and re-layouts  2.85 us (6%)
    pallas_call x1, Pallas kernels, shards(): pl.pallas_call(kernel, out_shape=jax.ShapeDtypeStruct((NLAT // LAT, CELLS...  43.6 us
    unnamed x1, local copies, waits for them, and re-layouts  1.58 us
    reshape x1, local copies, waits for them, and re-layouts, shards(): response.reshape(1, MODES)  1.27 us

profile of v1, /device:TPU:1, one launch (start us, length us, event | category | flops | bytes accessed | tf_op | source)
XLA Modules:
  0.0 46.5 jit_solution(17823151574151912655)
XLA Ops:
  0.0 1.3 %reshape.10.resp_ref = f32[1,640]{1,0:T(1,128)} reshape(f32[640]{0:T(1024)} %param.9) | data formatting | bytes 5120 | tf_op jit(solution)/shard_map/reshape | solution.py:433
  1.3 43.6 %shard_map.82 = f32[144,256]{1,0:T(8,128)} custom-call(f32[144,256]{1,0:T(8,128)} %bitcast.3, f32[1,640]{1,0:T(1,128)} %reshape.10.resp_ref, bf16[512,128]{1,0:T(8,128)(2,1)} %constant.12.clone.thi_ref, bf16[512,128]{1,0:T(8,128)(2,1)} %constant.13.clone.tlo_ref, f32[2,16,256]{2,1,0:T(8,128)} %constant.14.clone.tw_ref, f32[4,8,128]{2,1,0:T(8,128)} %constant.15.clone.geo_ref, ...), custom_call_target="tpu_custom_call" | custom-call | tf_op jit(solution)/shard_map/pallas_call | solution.py:402
  44.9 1.6 %copy.10 = f32[1,144,256]{2,1,0:T(8,128)} copy(f32[1,144,256]{2,1,0:T(8,128)} %bitcast.2) | data formatting | bytes 294912

commit v2 on v1

--- a/solution.py
+++ b/solution.py
@@ -21,6 +21,15 @@
 STARTS = [sum(MODES - DEV * t for t in range(i)) for i in range(SLOTS)]
 TALL = sum(MODES - DEV * t for t in range(SLOTS))
 WIDE = 640
+HOPS = (0, 1, 2, 1)
+FAR = sorted(
+    [(dy, dx, dz, dc) for dy in range(4) for dx in range(4) for dz in range(4) for dc in range(2)],
+    key=lambda o: (-HOPS[o[0]] - HOPS[o[1]] - HOPS[o[2]], -o[3]),
+)[: DEV - 1]
+FAR_LON = sorted(
+    [(dx, dz, dc) for dx in range(2) for dz in range(4) for dc in range(2)],
+    key=lambda o: (-o[0] - HOPS[o[1]], -o[2]),
+)[: LON - 1]
 bf16 = jnp.bfloat16
 f32 = jnp.float32
 
@@ -94,32 +103,61 @@
 
 
 def kernel(
-    h_ref, resp_ref, thi_ref, tlo_ref, tw_ref, geo_ref, wt_ref, lc_ref, o_ref,
+    h_hbm, resp_hbm, thi_hbm, tlo_hbm, tw_hbm, geo_hbm, wt_hbm, lc_ref, o_ref,
+    h_ref, resp_ref, thi_ref, tlo_ref, tw_ref, geo_ref, wt_ref,
     send_a, recv_a, zs, osc, send_b, recv_b, coef_a, coef_c, tall, phi, plo, fold, send_c, recv_c, vs, send_d, recv_d,
-    ssem, rsem,
+    ssem, rsem, lsem,
 ):
+    loads = [
+        pltpu.make_async_copy(source, target, lsem.at[n])
+        for n, (source, target) in enumerate(
+            [
+                (h_hbm, h_ref),
+                (geo_hbm, geo_ref),
+                (tw_hbm, tw_ref),
+                (thi_hbm, thi_ref),
+                (tlo_hbm, tlo_ref),
+                (wt_hbm, wt_ref),
+                (resp_hbm, resp_ref.at[pl.ds(0, SLOTS)]),
+            ]
+        )
+    ]
+    resp_ref[...] = jnp.zeros((8, 128), f32)
+    for load in loads:
+        load.start()
     lon = lax.axis_index("lon")
     lat = lax.axis_index("lat")
     me = lat * LON + lon
     south = lat // (LAT // 2)
     barrier = pltpu.get_barrier_semaphore()
 
-    def peer(p):
-        return {"lat": p // LON, "lon": p % LON}
-
-    def place(p):
-        return jnp.where(p < HALF, p, DEV + HALF - 1 - p)
-
-    def greet(step, carry):
-        pl.semaphore_signal(barrier, inc=1, device_id=peer(lax.rem(me + step, DEV)))
-        return carry
-
-    lax.fori_loop(1, DEV, greet, 0)
+    y, z, core = lat // 2, (lon // 2) % 4, lon % 2
+    x_low = lon // 8
+    x_all = (lat % 2) * 2 + x_low
+    at_y = [((y + d) % 4) * 2 for d in range(4)]
+    at_x = [(x_all + d) % 4 for d in range(4)]
+    at_x = [(v // 2, (v % 2) * 8) for v in at_x]
+    at_low = [((x_low + d) % 2) * 8 for d in range(2)]
+    at_z = [((z + d) % 4) * 2 for d in range(4)]
+    at_core = [core, 1 - core]
+    everyone = [(at_y[dy] + at_x[dx][0], at_x[dx][1] + at_z[dz] + at_core[dc]) for dy, dx, dz, dc in FAR]
+    row_peers = [at_low[dx] + at_z[dz] + at_core[dc] for dx, dz, dc in FAR_LON]
+
+    def place(a, b):
+        p = a * LON + b
+        return jnp.where(a < LAT // 2, p, DEV + HALF - 1 - p)
+
+    for a, b in everyone:
+        pl.semaphore_signal(barrier, inc=1, device_id={"lat": a, "lon": b})
+
+    loads[0].wait()
 
     def stage(block, carry):
         for r in range(ROWS):
             source = jnp.where(south == 1, ROWS - 1 - r, r)
-            send_a[block, r : r + 1, :] = h_ref[pl.ds(ROWS * block + source, 1), :]
+            line = h_ref[pl.ds(ROWS * block + source, 1), :]
+            send_a[block, r] = line[:, :128]
+            send_a[block, ROWS + r] = line[:, 128:]
         return carry
 
     lax.fori_loop(0, LON, stage, 0)
@@ -141,29 +179,7 @@
 
         lax.fori_loop(0, (MODES - DEV * i) // 32, coefficients, 0)
 
-    pl.semaphore_wait(barrier, DEV - 1)
-
-    def exchange_lon(send, recv, which):
-        def go(step, carry):
-            p = lax.rem(lon + step, LON)
-            pltpu.make_async_remote_copy(
-                send.at[p], recv.at[lon], ssem.at[which], rsem.at[which], device_id={"lat": lat, "lon": p}
-            ).start()
-            return carry
-
-        lax.fori_loop(1, LON, go, 0)
-        recv[lon] = send[lon]
-
-    def finish(send, recv, which, count):
-        every = pltpu.make_async_remote_copy(
-            send.at[pl.ds(0, count)], recv.at[pl.ds(0, count)], ssem.at[which], rsem.at[which],
-            device_id=peer(lax.rem(me + 1, DEV)),
-        )
-        every.wait_send()
-        every.wait_recv()
-
-    exchange_lon(send_a, recv_a, 0)
-
+    loads[1].wait()
     x = geo_ref[0]
     state = []
     for i in range(SLOTS):
@@ -197,6 +213,25 @@
 
         state = list(lax.fori_loop(0, DEV // 8, steps, tuple(state[:active])))
 
+    pl.semaphore_wait(barrier, DEV - 1)
+
+    def exchange_lon(send, recv, which):
+        for b in row_peers:
+            pltpu.make_async_remote_copy(
+                send.at[b], recv.at[lon], ssem.at[which], rsem.at[which], device_id={"lat": lat, "lon": b}
+            ).start()
+        recv[lon] = send[lon]
+
+    def finish(send, recv, which, count):
+        every = pltpu.make_async_remote_copy(
+            send.at[pl.ds(0, count)], recv.at[pl.ds(0, count)], ssem.at[which], rsem.at[which],
+            device_id={"lat": lat, "lon": row_peers[0]},
+        )
+        every.wait_send()
+        every.wait_recv()
+
+    exchange_lon(send_a, recv_a, 0)
+
     def halves(block, carry):
         row = pl.multiple_of(block * 16, 16)
         for j in range(5):
@@ -210,9 +245,10 @@
 
     finish(send_a, recv_a, 0, LON - 1)
 
+    loads[2].wait()
     for side in range(2):
         lanes = slice(side * 128, side * 128 + 128)
-        d = [recv_a[b, :, lanes] for b in range(LON)]
+        d = [recv_a[b, side * ROWS : side * ROWS + ROWS, 0, :] for b in range(LON)]
         even = {b: d[b] + d[16 - b] for b in range(1, 8)}
         odd = {b: d[b] - d[16 - b] for b in range(1, 8)}
         real = [None] * 9
@@ -239,15 +275,20 @@
             zs[rho, 0:ROWS, lanes] = zre
             zs[rho, 0:ROWS, CELLS + side * 128 : CELLS + side * 128 + 128] = zim
 
+    loads[3].wait()
+    loads[4].wait()
     zh, zl = split(zs[...].reshape(LON * 16, 2 * CELLS))
     thi = thi_ref[...]
     tlo = tlo_ref[...]
-    dims = (((1,), (0,)), ((), ()))
-    osc[...] = (
-        lax.dot_general(zh, thi, dims, preferred_element_type=f32)
-        + lax.dot_general(zl, thi, dims, preferred_element_type=f32)
-        + lax.dot_general(zh, tlo, dims, preferred_element_type=f32)
-    )
+    nn = (((1,), (0,)), ((), ()))
+    nt = (((1,), (1,)), ((), ()))
+
+    def product(high, low, other_high, other_low, dims):
+        count = high.shape[0]
+        both = lax.dot_general(jnp.concatenate([high, low], axis=0), other_high, dims, preferred_element_type=f32)
+        return both[:count] + both[count:] + lax.dot_general(high, other_low, dims, preferred_element_type=f32)
+
+    osc[...] = product(zh, zl, thi, tlo, nn)
 
     lane = lax.broadcasted_iota(jnp.int32, (LON, 128), 1)
     packed = [jnp.zeros((LON, 128), f32) for _ in range(LAT)]
@@ -262,21 +303,22 @@
         send_b[g * LON : (g + 1) * LON, 0, :] = packed[g]
 
     def exchange_all(send, recv, which, source, target):
-        def go(step, carry):
-            p = lax.rem(me + step, DEV)
+        for a, b in everyone:
             pltpu.make_async_remote_copy(
-                send.at[source(p)], recv.at[target], ssem.at[which], rsem.at[which], device_id=peer(p)
+                send.at[source(a, b)], recv.at[target], ssem.at[which], rsem.at[which], device_id={"lat": a, "lon": b}
             ).start()
-            return carry
-
-        lax.fori_loop(1, DEV, go, 0)
-        recv[target] = send[source(me)]
-
-    exchange_all(send_b, recv_b, 1, lambda p: p, place(me))
-
-    wide = jnp.concatenate([resp_ref[...], jnp.zeros((1, MODES), f32)], axis=1)
-    shifted = pltpu.roll(jnp.broadcast_to(wide, (8, 2 * MODES)), lax.rem(2 * MODES - me, 2 * MODES), axis=1)
-    response = jnp.concatenate([shifted[:1, DEV * i : MODES] for i in range(SLOTS)], axis=1)
+        recv[target] = send[source(lat, lon)]
+
+    exchange_all(send_b, recv_b, 1, lambda a, b: a * LON + b, place(lat, lon))
+
+    loads[5].wait()
+    loads[6].wait()
+    turned = pltpu.roll(resp_ref[...], lax.rem(DEV - me, DEV), axis=1)
+    within = lax.broadcasted_iota(jnp.int32, (SLOTS, 128), 1) < DEV - me
+    shifted = jnp.where(within, turned[0:SLOTS], turned[1 : SLOTS + 1])
+    response = jnp.concatenate(
+        [shifted[q : q + 1] for i in range(SLOTS) for q in range(i, SLOTS)], axis=1
+    )
     first = jnp.where(jnp.logical_and(lax.broadcasted_iota(jnp.int32, (1, TALL), 1) < MODES, me == 0), 1.0, 2.0)
     response = response * first
     row = lax.broadcasted_iota(jnp.int32, (32, TALL), 0)
@@ -309,18 +351,8 @@
     pad = jnp.zeros((6, WIDE), f32)
     lhs = jnp.concatenate([jnp.concatenate(evens, axis=1), pad, jnp.concatenate(odds, axis=1), pad], axis=0)
     lh, ll = split(lhs)
-    nt = (((1,), (1,)), ((), ()))
-    coefficients_ = (
-        lax.dot_general(lh, phi[...], nt, preferred_element_type=f32)
-        + lax.dot_general(ll, phi[...], nt, preferred_element_type=f32)
-        + lax.dot_general(lh, plo[...], nt, preferred_element_type=f32)
-    )
-    sh, sl = split(coefficients_ * gain)
-    synthesis = (
-        lax.dot_general(sh, phi[...], dims, preferred_element_type=f32)
-        + lax.dot_general(sl, phi[...], dims, preferred_element_type=f32)
-        + lax.dot_general(sh, plo[...], dims, preferred_element_type=f32)
-    )
+    sh, sl = split(product(lh, ll, phi[...], plo[...], nt) * gain)
+    synthesis = product(sh, sl, phi[...], plo[...], nn)
     fold[...] = jnp.zeros((128, 128), f32)
     for j in range(5):
         e = synthesis[0:10, j * 128 : (j + 1) * 128]
@@ -345,11 +377,7 @@
             value = jnp.where(mine, moved, value)
         gathered.append(value)
     gh, gl = split(jnp.concatenate(gathered, axis=0))
-    inverse = (
-        lax.dot_general(gh, thi, nt, preferred_element_type=f32)
-        + lax.dot_general(gl, thi, nt, preferred_element_type=f32)
-        + lax.dot_general(gh, tlo, nt, preferred_element_type=f32)
-    )
+    inverse = product(gh, gl, thi, tlo, nt)
     for c in range(4):
         vs[c] = inverse[:, c * 128 : (c + 1) * 128]
 
@@ -364,6 +392,7 @@
             vim = vs[2 + side, pl.ds(rho, ROWS, stride=16), :]
             real.append(vre * tc - vim * ts)
             imag.append(None if rho % 8 == 0 else vre * ts + vim * tc)
+        mine = slice(side * ROWS, side * ROWS + ROWS)
         ure = {rho: real[rho] + real[16 - rho] for rho in range(1, 8)}
         uim = {rho: imag[rho] - imag[16 - rho] for rho in range(1, 8)}
         for b in range(5):
@@ -373,13 +402,13 @@
             go = combine([(ure[q], cosine(q * b)) for q in (1, 3, 5, 7)])
             he = combine([(uim[q], sine(q * b)) for q in (2, 4, 6)])
             ho = combine([(uim[q], sine(q * b)) for q in (1, 3, 5, 7)])
-            send_d[b, :, lanes] = (ge + go) - (he + ho)
+            send_d[b, mine, 0, :] = (ge + go) - (he + ho)
             if b > 0:
-                send_d[16 - b, :, lanes] = (ge + go) + (he + ho)
+                send_d[16 - b, mine, 0, :] = (ge + go) + (he + ho)
             if b < 4:
-                send_d[8 - b, :, lanes] = (ge - go) - (ho - he)
+                send_d[8 - b, mine, 0, :] = (ge - go) - (ho - he)
                 if b > 0:
-                    send_d[8 + b, :, lanes] = (ge - go) + (ho - he)
+                    send_d[8 + b, mine, 0, :] = (ge - go) + (ho - he)
 
     exchange_lon(send_d, recv_d, 3)
     finish(send_d, recv_d, 3, LON - 1)
@@ -387,7 +416,8 @@
     def unstage(block, carry):
         for r in range(ROWS):
             target = jnp.where(south == 1, ROWS - 1 - r, r)
-            o_ref[pl.ds(ROWS * block + target, 1), :] = recv_d[block, r : r + 1, :]
+            line = jnp.concatenate([recv_d[block, r], recv_d[block, ROWS + r]], axis=1)
+            o_ref[pl.ds(ROWS * block + target, 1), :] = line
         return carry
 
     lax.fori_loop(0, LON, unstage, 0)
@@ -397,14 +427,22 @@
     high, low, twiddle, geometry, weights, first = constants()
     vmem = pl.BlockSpec(memory_space=pltpu.VMEM)
     smem = pl.BlockSpec(memory_space=pltpu.SMEM)
-    blocks = pltpu.VMEM((LON, ROWS, CELLS), f32)
+    hbm = pl.BlockSpec(memory_space=pltpu.HBM)
+    blocks = pltpu.VMEM((LON, 2 * ROWS, 1, 128), f32)
     rows = pltpu.VMEM((DEV, 1, 128), f32)
     out = pl.pallas_call(
         kernel,
         out_shape=jax.ShapeDtypeStruct((NLAT // LAT, CELLS), f32),
-        in_specs=[vmem] * 7 + [smem],
+        in_specs=[hbm] * 7 + [smem],
         out_specs=vmem,
         scratch_shapes=[
+            pltpu.VMEM((NLAT // LAT, CELLS), f32),
+            pltpu.VMEM((8, 128), f32),
+            pltpu.VMEM((2 * CELLS, 128), bf16),
+            pltpu.VMEM((2 * CELLS, 128), bf16),
+            pltpu.VMEM((2, LON, CELLS), f32),
+            pltpu.VMEM((4, 8, 128), f32),
+            pltpu.VMEM((HALF, 128), f32),
             blocks,
             blocks,
             pltpu.VMEM((LON, 16, 2 * CELLS), f32),
@@ -424,13 +462,14 @@
             blocks,
             pltpu.SemaphoreType.DMA((4,)),
             pltpu.SemaphoreType.DMA((4,)),
+            pltpu.SemaphoreType.DMA((7,)),
         ],
         compiler_params=pltpu.CompilerParams(
             collective_id=0, has_side_effects=True, vmem_limit_bytes=60 * 1024 * 1024
         ),
     )(
         height.reshape(NLAT // LAT, CELLS),
-        response.reshape(1, MODES),
+        response.reshape(SLOTS, 128),
         jnp.asarray(high),
         jnp.asarray(low),
         jnp.asarray(twiddle),

time: 46.7 us -> 38.7 us (0.83)
  Pallas kernels: 43.6 us -> 37 us
  local copies, waits for them, and re-layouts: 2.85 us -> 1.58 us
    pallas_call x1, Pallas kernels: 43.6 us -> 37 us  [shards(): pl.pallas_call(kernel, out_shape=jax.ShapeDtypeStruct((NLAT // LAT, CELLS...]
    reshape x1 -> x0, local copies, waits for them, and re-layouts: 1.27 us -> none  [shards(): response.reshape(1, MODES)]
where the time goes in v2:
time: 38.7 us; the launch traced here: 38.6 us
  Pallas kernels  37 us (96%)
  local copies, waits for them, and re-layouts  1.58 us (4%)
    pallas_call x1, Pallas kernels, shards(): pl.pallas_call(kernel, out_shape=jax.ShapeDtypeStruct((NLAT // LAT, CELLS...  37 us
    unnamed x1, local copies, waits for them, and re-layouts  1.58 us

profile of v2, /device:TPU:1, one launch (start us, length us, event | category | flops | bytes accessed | tf_op | source)
XLA Modules:
  0.0 38.6 jit_solution(7739340708218089203)
XLA Ops:
  0.0 37.0 %shard_map.82 = f32[144,256]{1,0:T(8,128)} custom-call(f32[144,256]{1,0:T(8,128)} %bitcast.4, f32[5,128]{1,0:T(8,128)} %bitcast.5, bf16[512,128]{1,0:T(8,128)(2,1)} %constant.12.clone.thi_hbm, bf16[512,128]{1,0:T(8,128)(2,1)} %constant.13.clone.tlo_hbm, f32[2,16,256]{2,1,0:T(8,128)} %constant.14.clone.tw_hbm, f32[4,8,128]{2,1,0:T(8,128)} %constant.15.clone.geo_hbm, ...), custom_call_target="tpu_custom_call" | custom-call | tf_op jit(solution)/shard_map/pallas_call | solution.py:433
  37.0 1.6 %copy.10 = f32[1,144,256]{2,1,0:T(8,128)} copy(f32[1,144,256]{2,1,0:T(8,128)} %bitcast.3) | data formatting | bytes 294912

commit v3 on v2

--- a/solution.py
+++ b/solution.py
@@ -103,10 +103,10 @@
 
 
 def kernel(
-    h_hbm, resp_hbm, thi_hbm, tlo_hbm, tw_hbm, geo_hbm, wt_hbm, lc_ref, o_ref,
+    h_hbm, resp_hbm, thi_hbm, tlo_hbm, tw_hbm, geo_hbm, wt_hbm, lc_ref, o_hbm,
     h_ref, resp_ref, thi_ref, tlo_ref, tw_ref, geo_ref, wt_ref,
-    send_a, recv_a, zs, osc, send_b, recv_b, coef_a, coef_c, tall, phi, plo, fold, send_c, recv_c, vs, send_d, recv_d,
-    ssem, rsem, lsem,
+    send_a, recv_a, zs, osc, send_b, recv_b, coef_a, coef_c, tall, phi, plo, phi_t, plo_t, fold, send_c, recv_c, vs, send_d, recv_d,
+    out_ref, ssem, rsem, lsem,
 ):
     loads = [
         pltpu.make_async_copy(source, target, lsem.at[n])
@@ -147,7 +147,11 @@
         p = a * LON + b
         return jnp.where(a < LAT // 2, p, DEV + HALF - 1 - p)
 
-    for a, b in everyone:
+    greeted = [(lat, b) for b in row_peers]
+    x_high = lat % 2
+    same, mirror = lon, (1 - x_low) * 8 + z * 2 + core
+    greeted += [(at_y[d] + 1 - x_high, mirror) for d in (2, 1, 3, 0)] + [(at_y[d] + x_high, same) for d in (2, 1, 3)]
+    for a, b in greeted:
         pl.semaphore_signal(barrier, inc=1, device_id={"lat": a, "lon": b})
 
     loads[0].wait()
@@ -156,8 +160,8 @@
         for r in range(ROWS):
             source = jnp.where(south == 1, ROWS - 1 - r, r)
             line = h_ref[pl.ds(ROWS * block + source, 1), :]
-            send_a[block, r] = line[:, :128]
-            send_a[block, ROWS + r] = line[:, 128:]
+            send_a[0, block, r] = line[:, :128]
+            send_a[1, block, r] = line[:, 128:]
         return carry
 
     lax.fori_loop(0, LON, stage, 0)
@@ -178,6 +182,26 @@
             return carry
 
         lax.fori_loop(0, (MODES - DEV * i) // 32, coefficients, 0)
+
+    pl.semaphore_wait(barrier, len(greeted))
+
+    def exchange_lon(send, recv, which):
+        for b in row_peers:
+            pltpu.make_async_remote_copy(
+                send.at[b], recv.at[lon], ssem.at[which], rsem.at[which], device_id={"lat": lat, "lon": b}
+            ).start()
+        recv[lon] = send[lon]
+
+    def finish(send, recv, which, count):
+        every = pltpu.make_async_remote_copy(
+            send.at[pl.ds(0, count)], recv.at[pl.ds(0, count)], ssem.at[which], rsem.at[which],
+            device_id={"lat": lat, "lon": row_peers[0]},
+        )
+        every.wait_send()
+        every.wait_recv()
+
+    for side in range(2):
+        exchange_lon(send_a.at[side], recv_a.at[side], side)
 
     loads[1].wait()
     x = geo_ref[0]
@@ -213,42 +237,25 @@
 
         state = list(lax.fori_loop(0, DEV // 8, steps, tuple(state[:active])))
 
-    pl.semaphore_wait(barrier, DEV - 1)
-
-    def exchange_lon(send, recv, which):
-        for b in row_peers:
-            pltpu.make_async_remote_copy(
-                send.at[b], recv.at[lon], ssem.at[which], rsem.at[which], device_id={"lat": lat, "lon": b}
-            ).start()
-        recv[lon] = send[lon]
-
-    def finish(send, recv, which, count):
-        every = pltpu.make_async_remote_copy(
-            send.at[pl.ds(0, count)], recv.at[pl.ds(0, count)], ssem.at[which], rsem.at[which],
-            device_id={"lat": lat, "lon": row_peers[0]},
-        )
-        every.wait_send()
-        every.wait_recv()
-
-    exchange_lon(send_a, recv_a, 0)
-
     def halves(block, carry):
-        row = pl.multiple_of(block * 16, 16)
+        row = pl.multiple_of(block * 128, 128)
         for j in range(5):
-            value = tall[pl.ds(row * 8 + j, 16, stride=8), :]
+            value = tall[pl.ds(row * 8 + j, 128, stride=8), :]
             high, low = split(value)
-            phi[pl.ds(row, 16), j * 128 : (j + 1) * 128] = high
-            plo[pl.ds(row, 16), j * 128 : (j + 1) * 128] = low
+            phi[pl.ds(row, 128), j * 128 : (j + 1) * 128] = high
+            plo[pl.ds(row, 128), j * 128 : (j + 1) * 128] = low
+            high, low = high.T, low.T
+            phi_t[j * 128 : (j + 1) * 128, pl.ds(row, 128)] = high
+            plo_t[j * 128 : (j + 1) * 128, pl.ds(row, 128)] = low
         return carry
 
-    lax.fori_loop(0, TALL // 16, halves, 0)
-
-    finish(send_a, recv_a, 0, LON - 1)
+    lax.fori_loop(0, TALL // 128, halves, 0)
 
     loads[2].wait()
     for side in range(2):
         lanes = slice(side * 128, side * 128 + 128)
-        d = [recv_a[b, side * ROWS : side * ROWS + ROWS, 0, :] for b in range(LON)]
+        finish(send_a.at[side], recv_a.at[side], side, LON - 1)
+        d = [recv_a[side, b, :, 0, :] for b in range(LON)]
         even = {b: d[b] + d[16 - b] for b in range(1, 8)}
         odd = {b: d[b] - d[16 - b] for b in range(1, 8)}
         real = [None] * 9
@@ -309,7 +316,7 @@
             ).start()
         recv[target] = send[source(lat, lon)]
 
-    exchange_all(send_b, recv_b, 1, lambda a, b: a * LON + b, place(lat, lon))
+    exchange_all(send_b, recv_b, 2, lambda a, b: a * LON + b, place(lat, lon))
 
     loads[5].wait()
     loads[6].wait()
@@ -330,7 +337,7 @@
     keep = jnp.logical_or(row == wanted, row == wanted + 1)
     gain = jnp.where(keep, response, 0.0)
 
-    finish(send_b, recv_b, 1, DEV - 1)
+    finish(send_b, recv_b, 2, DEV - 1)
 
     north = recv_b[0:HALF, 0, :]
     southern = recv_b[HALF:DEV, 0, :]
@@ -351,7 +358,7 @@
     pad = jnp.zeros((6, WIDE), f32)
     lhs = jnp.concatenate([jnp.concatenate(evens, axis=1), pad, jnp.concatenate(odds, axis=1), pad], axis=0)
     lh, ll = split(lhs)
-    sh, sl = split(product(lh, ll, phi[...], plo[...], nt) * gain)
+    sh, sl = split(product(lh, ll, phi_t[...], plo_t[...], nn) * gain)
     synthesis = product(sh, sl, phi[...], plo[...], nn)
     fold[...] = jnp.zeros((128, 128), f32)
     for j in range(5):
@@ -363,8 +370,8 @@
             fold[20 * j + 10 : 20 * j + 20, :] = jnp.where(left, pltpu.roll(n, HALF, axis=1), s)
     send_c[:, 0, :] = fold[...].T
 
-    exchange_all(send_c, recv_c, 2, place, me)
-    finish(send_c, recv_c, 2, DEV - 1)
+    exchange_all(send_c, recv_c, 3, place, me)
+    finish(send_c, recv_c, 3, DEV - 1)
 
     pieces = [recv_c[g * LON : (g + 1) * LON, 0, :] for g in range(LAT)]
     gathered = []
@@ -392,9 +399,12 @@
             vim = vs[2 + side, pl.ds(rho, ROWS, stride=16), :]
             real.append(vre * tc - vim * ts)
             imag.append(None if rho % 8 == 0 else vre * ts + vim * tc)
-        mine = slice(side * ROWS, side * ROWS + ROWS)
         ure = {rho: real[rho] + real[16 - rho] for rho in range(1, 8)}
         uim = {rho: imag[rho] - imag[16 - rho] for rho in range(1, 8)}
+        def put(b, value, side=side):
+            for r in range(ROWS):
+                send_d[side, b, jnp.where(south == 1, ROWS - 1 - r, r)] = value[r : r + 1]
+
         for b in range(5):
             ge = combine(
                 [(real[0], 1.0), (real[8], 1.0 - 2.0 * (b % 2))] + [(ure[q], cosine(q * b)) for q in (2, 4, 6)]
@@ -402,39 +412,39 @@
             go = combine([(ure[q], cosine(q * b)) for q in (1, 3, 5, 7)])
             he = combine([(uim[q], sine(q * b)) for q in (2, 4, 6)])
             ho = combine([(uim[q], sine(q * b)) for q in (1, 3, 5, 7)])
-            send_d[b, mine, 0, :] = (ge + go) - (he + ho)
+            put(b, (ge + go) - (he + ho))
             if b > 0:
-                send_d[16 - b, mine, 0, :] = (ge + go) + (he + ho)
+                put(16 - b, (ge + go) + (he + ho))
             if b < 4:
-                send_d[8 - b, mine, 0, :] = (ge - go) - (ho - he)
+                put(8 - b, (ge - go) - (ho - he))
                 if b > 0:
-                    send_d[8 + b, mine, 0, :] = (ge - go) + (ho - he)
-
-    exchange_lon(send_d, recv_d, 3)
-    finish(send_d, recv_d, 3, LON - 1)
-
-    def unstage(block, carry):
-        for r in range(ROWS):
-            target = jnp.where(south == 1, ROWS - 1 - r, r)
-            line = jnp.concatenate([recv_d[block, r], recv_d[block, ROWS + r]], axis=1)
-            o_ref[pl.ds(ROWS * block + target, 1), :] = line
-        return carry
-
-    lax.fori_loop(0, LON, unstage, 0)
+                    put(8 + b, (ge - go) + (ho - he))
+        exchange_lon(send_d.at[side], recv_d.at[side], 4 + side)
+
+    stores = []
+    for side in range(2):
+        lanes = slice(side * 128, side * 128 + 128)
+        finish(send_d.at[side], recv_d.at[side], 4 + side, LON - 1)
+        for b in range(LON):
+            out_ref[ROWS * b : ROWS * b + ROWS, lanes] = recv_d[side, b, :, 0, :]
+        store = pltpu.make_async_copy(out_ref.at[:, lanes], o_hbm.at[:, lanes], lsem.at[7 + side])
+        store.start()
+        stores.append(store)
+    for store in stores:
+        store.wait()
 
 
 def shards(height, response):
     high, low, twiddle, geometry, weights, first = constants()
-    vmem = pl.BlockSpec(memory_space=pltpu.VMEM)
     smem = pl.BlockSpec(memory_space=pltpu.SMEM)
     hbm = pl.BlockSpec(memory_space=pltpu.HBM)
-    blocks = pltpu.VMEM((LON, 2 * ROWS, 1, 128), f32)
+    blocks = pltpu.VMEM((2, LON, ROWS, 1, 128), f32)
     rows = pltpu.VMEM((DEV, 1, 128), f32)
     out = pl.pallas_call(
         kernel,
         out_shape=jax.ShapeDtypeStruct((NLAT // LAT, CELLS), f32),
         in_specs=[hbm] * 7 + [smem],
-        out_specs=vmem,
+        out_specs=hbm,
         scratch_shapes=[
             pltpu.VMEM((NLAT // LAT, CELLS), f32),
             pltpu.VMEM((8, 128), f32),
@@ -454,15 +464,18 @@
             pltpu.VMEM((TALL * 8, 128), f32),
             pltpu.VMEM((TALL, WIDE), bf16),
             pltpu.VMEM((TALL, WIDE), bf16),
+            pltpu.VMEM((WIDE, TALL), bf16),
+            pltpu.VMEM((WIDE, TALL), bf16),
             pltpu.VMEM((128, 128), f32),
             rows,
             rows,
             pltpu.VMEM((4, ROWS * LON, 128), f32),
             blocks,
             blocks,
-            pltpu.SemaphoreType.DMA((4,)),
-            pltpu.SemaphoreType.DMA((4,)),
-            pltpu.SemaphoreType.DMA((7,)),
+            pltpu.VMEM((NLAT // LAT, CELLS), f32),
+            pltpu.SemaphoreType.DMA((6,)),
+            pltpu.SemaphoreType.DMA((6,)),
+            pltpu.SemaphoreType.DMA((9,)),
         ],
         compiler_params=pltpu.CompilerParams(
             collective_id=0, has_side_effects=True, vmem_limit_bytes=60 * 1024 * 1024

time: 38.7 us -> 36.7 us (0.948)
  Pallas kernels: 37 us -> 34.9 us
    pallas_call x1, Pallas kernels: 37 us -> 34.9 us  [shards(): pl.pallas_call(kernel, out_shape=jax.ShapeDtypeStruct((NLAT // LAT, CELLS...]
where the time goes in v3:
time: 36.7 us; the launch traced here: 36.5 us
  Pallas kernels  34.9 us (95%)
  local copies, waits for them, and re-layouts  1.58 us (4%)
    pallas_call x1, Pallas kernels, shards(): pl.pallas_call(kernel, out_shape=jax.ShapeDtypeStruct((NLAT // LAT, CELLS...  34.9 us
    unnamed x1, local copies, waits for them, and re-layouts  1.58 us

profile of v3, /device:TPU:1, one launch (start us, length us, event | category | flops | bytes accessed | tf_op | source)
XLA Modules:
  0.0 36.5 jit_solution(5541054930053751111)
XLA Ops:
  0.0 34.9 %shard_map.82 = f32[144,256]{1,0:T(8,128)} custom-call(f32[144,256]{1,0:T(8,128)} %bitcast.4, f32[5,128]{1,0:T(8,128)} %bitcast.5, bf16[512,128]{1,0:T(8,128)(2,1)} %constant.12.clone.thi_hbm, bf16[512,128]{1,0:T(8,128)(2,1)} %constant.13.clone.tlo_hbm, f32[2,16,256]{2,1,0:T(8,128)} %constant.14.clone.tw_hbm, f32[4,8,128]{2,1,0:T(8,128)} %constant.15.clone.geo_hbm, ...), custom_call_target="tpu_custom_call" | custom-call | tf_op jit(solution)/shard_map/pallas_call | solution.py:443
  34.9 1.6 %copy.10 = f32[1,144,256]{2,1,0:T(8,128)} copy(f32[1,144,256]{2,1,0:T(8,128)} %bitcast.3) | data formatting | bytes 294912

commit v4 on v3

--- a/solution.py
+++ b/solution.py
@@ -49,7 +49,7 @@
     low = (table - high.astype(np.float64)).astype(np.float32).astype(bf16)
     angle = 2 * np.pi * np.arange(LON)[:, None] * t[None, :] / NLON
     twiddle = np.stack([np.cos(angle), np.sin(angle)]).astype(np.float32)
-    geometry = np.zeros((4, 8, 128), np.float32)
+    geometry = np.zeros((5, 8, 128), np.float32)
     for chunk in range(5):
         for lane in range(128):
             r = 2 * chunk + lane // HALF
@@ -57,7 +57,7 @@
                 theta = np.pi * (ROWS * (lane % HALF) + r + 0.5) / NLAT
                 log_sine = np.log2(np.sin(theta))
                 coarse = np.round(log_sine * 1024) / 1024
-                geometry[:, chunk, lane] = np.cos(theta), coarse, log_sine - coarse, 1.0
+                geometry[:4, chunk, lane] = np.cos(theta), coarse, log_sine - coarse, 1.0
     weights = np.zeros((HALF, 128), np.float32)
     for r in range(ROWS):
         theta = np.pi * (ROWS * np.arange(HALF) + r + 0.5) / NLAT
@@ -68,7 +68,8 @@
         / math.log(2)
         for m in range(MODES)
     ]
-    return high, low, twiddle, geometry, weights, np.asarray(first, np.float32)
+    geometry[4, :SLOTS] = np.reshape(first, (SLOTS, DEV))
+    return high, low, twiddle, geometry, weights
 
 
 def split(x):
@@ -103,10 +104,10 @@
 
 
 def kernel(
-    h_hbm, resp_hbm, thi_hbm, tlo_hbm, tw_hbm, geo_hbm, wt_hbm, lc_ref, o_hbm,
+    h_hbm, resp_hbm, thi_hbm, tlo_hbm, tw_hbm, geo_hbm, wt_hbm, o_hbm,
     h_ref, resp_ref, thi_ref, tlo_ref, tw_ref, geo_ref, wt_ref,
     send_a, recv_a, zs, osc, send_b, recv_b, coef_a, coef_c, tall, phi, plo, phi_t, plo_t, fold, send_c, recv_c, vs, send_d, recv_d,
-    out_ref, ssem, rsem, lsem,
+    ssem, rsem, lsem,
 ):
     loads = [
         pltpu.make_async_copy(source, target, lsem.at[n])
@@ -205,11 +206,12 @@
 
     loads[1].wait()
     x = geo_ref[0]
+    starts = pltpu.roll(geo_ref[4], lax.rem(DEV - me, DEV), axis=1)
     state = []
     for i in range(SLOTS):
         m = (DEV * i + me).astype(f32)
         coarse = m * geo_ref[1]
-        fine = m * geo_ref[2] + lc_ref[DEV * i + me]
+        fine = m * geo_ref[2] + jnp.broadcast_to(starts[i : i + 1, 0:1], (8, 128))
         count = jnp.maximum(jnp.ceil((-84.0 - (coarse + fine)) * (1.0 / 64.0)), 0.0)
         value = jnp.exp2((coarse + 64.0 * count) + fine) * geo_ref[3]
         state.append((jnp.zeros_like(value), value, count))
@@ -236,20 +238,6 @@
             return tuple(new)
 
         state = list(lax.fori_loop(0, DEV // 8, steps, tuple(state[:active])))
-
-    def halves(block, carry):
-        row = pl.multiple_of(block * 128, 128)
-        for j in range(5):
-            value = tall[pl.ds(row * 8 + j, 128, stride=8), :]
-            high, low = split(value)
-            phi[pl.ds(row, 128), j * 128 : (j + 1) * 128] = high
-            plo[pl.ds(row, 128), j * 128 : (j + 1) * 128] = low
-            high, low = high.T, low.T
-            phi_t[j * 128 : (j + 1) * 128, pl.ds(row, 128)] = high
-            plo_t[j * 128 : (j + 1) * 128, pl.ds(row, 128)] = low
-        return carry
-
-    lax.fori_loop(0, TALL // 128, halves, 0)
 
     loads[2].wait()
     for side in range(2):
@@ -307,16 +295,31 @@
             moved = pltpu.roll(value, shift, axis=1) if shift else value
             packed[g] = jnp.where(mine, moved, packed[g])
     for g in range(LAT):
-        send_b[g * LON : (g + 1) * LON, 0, :] = packed[g]
+        send_b[g * LON : (g + 1) * LON, :] = packed[g]
 
     def exchange_all(send, recv, which, source, target):
         for a, b in everyone:
             pltpu.make_async_remote_copy(
-                send.at[source(a, b)], recv.at[target], ssem.at[which], rsem.at[which], device_id={"lat": a, "lon": b}
+                send.at[pl.ds(source(a, b), 1)], recv.at[pl.ds(target, 1)], ssem.at[which], rsem.at[which],
+                device_id={"lat": a, "lon": b},
             ).start()
-        recv[target] = send[source(lat, lon)]
+        recv[pl.ds(target, 1), :] = send[pl.ds(source(lat, lon), 1), :]
 
     exchange_all(send_b, recv_b, 2, lambda a, b: a * LON + b, place(lat, lon))
+
+    def halves(block, carry):
+        row = pl.multiple_of(block * 128, 128)
+        for j in range(5):
+            value = tall[pl.ds(row * 8 + j, 128, stride=8), :]
+            high, low = split(value)
+            phi[pl.ds(row, 128), j * 128 : (j + 1) * 128] = high
+            plo[pl.ds(row, 128), j * 128 : (j + 1) * 128] = low
+            high, low = high.T, low.T
+            phi_t[j * 128 : (j + 1) * 128, pl.ds(row, 128)] = high
+            plo_t[j * 128 : (j + 1) * 128, pl.ds(row, 128)] = low
+        return carry
+
+    lax.fori_loop(0, TALL // 128, halves, 0)
 
     loads[5].wait()
     loads[6].wait()
@@ -339,8 +342,8 @@
 
     finish(send_b, recv_b, 2, DEV - 1)
 
-    north = recv_b[0:HALF, 0, :]
-    southern = recv_b[HALF:DEV, 0, :]
+    north = recv_b[0:HALF, :]
+    southern = recv_b[HALF:DEV, :]
     weights = wt_ref[...]
     folded = jnp.concatenate([(north + southern) * weights, (north - southern) * weights], axis=0)
     fold[...] = folded.T
@@ -368,12 +371,12 @@
         fold[20 * j : 20 * j + 10, :] = jnp.where(left, n, pltpu.roll(s, HALF, axis=1))
         if j < 4:
             fold[20 * j + 10 : 20 * j + 20, :] = jnp.where(left, pltpu.roll(n, HALF, axis=1), s)
-    send_c[:, 0, :] = fold[...].T
+    send_c[...] = fold[...].T
 
     exchange_all(send_c, recv_c, 3, place, me)
     finish(send_c, recv_c, 3, DEV - 1)
 
-    pieces = [recv_c[g * LON : (g + 1) * LON, 0, :] for g in range(LAT)]
+    pieces = [recv_c[g * LON : (g + 1) * LON, :] for g in range(LAT)]
     gathered = []
     for r in range(ROWS):
         value = jnp.zeros((LON, 128), f32)
@@ -403,7 +406,8 @@
         uim = {rho: imag[rho] - imag[16 - rho] for rho in range(1, 8)}
         def put(b, value, side=side):
             for r in range(ROWS):
-                send_d[side, b, jnp.where(south == 1, ROWS - 1 - r, r)] = value[r : r + 1]
+                target = ROWS * b + jnp.where(south == 1, ROWS - 1 - r, r)
+                send_d[side, pl.ds(target, 1), :] = value[r : r + 1]
 
         for b in range(5):
             ge = combine(
@@ -419,15 +423,19 @@
                 put(8 - b, (ge - go) - (ho - he))
                 if b > 0:
                     put(8 + b, (ge - go) + (ho - he))
-        exchange_lon(send_d.at[side], recv_d.at[side], 4 + side)
+        for b in row_peers:
+            pltpu.make_async_remote_copy(
+                send_d.at[side, pl.ds(ROWS * b, ROWS)], recv_d.at[side, pl.ds(ROWS * lon, ROWS)],
+                ssem.at[4 + side], rsem.at[4 + side], device_id={"lat": lat, "lon": b},
+            ).start()
+        for r in range(ROWS):
+            recv_d[side, pl.ds(ROWS * lon + r, 1), :] = send_d[side, pl.ds(ROWS * lon + r, 1), :]
 
     stores = []
     for side in range(2):
         lanes = slice(side * 128, side * 128 + 128)
-        finish(send_d.at[side], recv_d.at[side], 4 + side, LON - 1)
-        for b in range(LON):
-            out_ref[ROWS * b : ROWS * b + ROWS, lanes] = recv_d[side, b, :, 0, :]
-        store = pltpu.make_async_copy(out_ref.at[:, lanes], o_hbm.at[:, lanes], lsem.at[7 + side])
+        finish(send_d.at[side], recv_d.at[side], 4 + side, ROWS * (LON - 1))
+        store = pltpu.make_async_copy(recv_d.at[side], o_hbm.at[:, lanes], lsem.at[7 + side])
         store.start()
         stores.append(store)
     for store in stores:
@@ -435,15 +443,14 @@
 
 
 def shards(height, response):
-    high, low, twiddle, geometry, weights, first = constants()
-    smem = pl.BlockSpec(memory_space=pltpu.SMEM)
+    high, low, twiddle, geometry, weights = constants()
     hbm = pl.BlockSpec(memory_space=pltpu.HBM)
     blocks = pltpu.VMEM((2, LON, ROWS, 1, 128), f32)
-    rows = pltpu.VMEM((DEV, 1, 128), f32)
+    rows = pltpu.VMEM((DEV, 128), f32)
     out = pl.pallas_call(
         kernel,
         out_shape=jax.ShapeDtypeStruct((NLAT // LAT, CELLS), f32),
-        in_specs=[hbm] * 7 + [smem],
+        in_specs=[hbm] * 7,
         out_specs=hbm,
         scratch_shapes=[
             pltpu.VMEM((NLAT // LAT, CELLS), f32),
@@ -451,7 +458,7 @@
             pltpu.VMEM((2 * CELLS, 128), bf16),
             pltpu.VMEM((2 * CELLS, 128), bf16),
             pltpu.VMEM((2, LON, CELLS), f32),
-            pltpu.VMEM((4, 8, 128), f32),
+            pltpu.VMEM((5, 8, 128), f32),
             pltpu.VMEM((HALF, 128), f32),
             blocks,
             blocks,
@@ -470,9 +477,8 @@
             rows,
             rows,
             pltpu.VMEM((4, ROWS * LON, 128), f32),
-            blocks,
-            blocks,
-            pltpu.VMEM((NLAT // LAT, CELLS), f32),
+            pltpu.VMEM((2, NLAT // LAT, 128), f32),
+            pltpu.VMEM((2, NLAT // LAT, 128), f32),
             pltpu.SemaphoreType.DMA((6,)),
             pltpu.SemaphoreType.DMA((6,)),
             pltpu.SemaphoreType.DMA((9,)),
@@ -488,7 +494,6 @@
         jnp.asarray(twiddle),
         jnp.asarray(geometry),
         jnp.asarray(weights),
-        jnp.asarray(first),
     )
     return out.reshape(height.shape)
 

time: 36.7 us -> 34.4 us (0.937)
  Pallas kernels: 34.9 us -> 32.7 us
    pallas_call x1, Pallas kernels: 34.9 us -> 32.7 us  [shards(): pl.pallas_call(kernel, out_shape=jax.ShapeDtypeStruct((NLAT // LAT, CELLS...]
where the time goes in v4:
time: 34.4 us; the launch traced here: 34.3 us
  Pallas kernels  32.7 us (95%)
  local copies, waits for them, and re-layouts  1.58 us (5%)
    pallas_call x1, Pallas kernels, shards(): pl.pallas_call(kernel, out_shape=jax.ShapeDtypeStruct((NLAT // LAT, CELLS...  32.7 us
    unnamed x1, local copies, waits for them, and re-layouts  1.58 us

profile of v4, /device:TPU:1, one launch (start us, length us, event | category | flops | bytes accessed | tf_op | source)
XLA Modules:
  0.0 34.3 jit_solution(15987207513100718177)
XLA Ops:
  0.0 32.7 %shard_map.73 = f32[144,256]{1,0:T(8,128)} custom-call(f32[144,256]{1,0:T(8,128)} %bitcast.4, f32[5,128]{1,0:T(8,128)} %bitcast.5, bf16[512,128]{1,0:T(8,128)(2,1)} %constant.10.clone.thi_hbm, bf16[512,128]{1,0:T(8,128)(2,1)} %constant.11.clone.tlo_hbm, f32[2,16,256]{2,1,0:T(8,128)} %constant.12.clone.tw_hbm, f32[5,8,128]{2,1,0:T(8,128)} %constant.13.clone.geo_hbm, ...), custom_call_target="tpu_custom_call" | custom-call | tf_op jit(solution)/shard_map/pallas_call | solution.py:450
  32.7 1.6 %copy.9 = f32[1,144,256]{2,1,0:T(8,128)} copy(f32[1,144,256]{2,1,0:T(8,128)} %bitcast.3) | data formatting | bytes 294912

commit v5 on v4

--- a/solution.py
+++ b/solution.py
@@ -45,8 +45,6 @@
             table[CELLS:, column] = np.sin(angle)
             table[:CELLS, column + 1] = -np.sin(angle)
             table[CELLS:, column + 1] = np.cos(angle)
-    high = table.astype(np.float32).astype(bf16)
-    low = (table - high.astype(np.float64)).astype(np.float32).astype(bf16)
     angle = 2 * np.pi * np.arange(LON)[:, None] * t[None, :] / NLON
     twiddle = np.stack([np.cos(angle), np.sin(angle)]).astype(np.float32)
     geometry = np.zeros((5, 8, 128), np.float32)
@@ -69,7 +67,9 @@
         for m in range(MODES)
     ]
     geometry[4, :SLOTS] = np.reshape(first, (SLOTS, DEV))
-    return high, low, twiddle, geometry, weights
+    twiddle = twiddle.reshape(2, LON, 2, 128).transpose(0, 2, 1, 3).reshape(4 * LON, 128)
+    parts = [table.astype(np.float32), twiddle, geometry.reshape(40, 128), weights]
+    return np.concatenate(parts)
 
 
 def split(x):
@@ -104,8 +104,8 @@
 
 
 def kernel(
-    h_hbm, resp_hbm, thi_hbm, tlo_hbm, tw_hbm, geo_hbm, wt_hbm, o_hbm,
-    h_ref, resp_ref, thi_ref, tlo_ref, tw_ref, geo_ref, wt_ref,
+    h_hbm, resp_hbm, fixed_hbm, o_ref,
+    h_ref, resp_ref, table_ref, tw_ref, geo_ref, wt_ref,
     send_a, recv_a, zs, osc, send_b, recv_b, coef_a, coef_c, tall, phi, plo, phi_t, plo_t, fold, send_c, recv_c, vs, send_d, recv_d,
     ssem, rsem, lsem,
 ):
@@ -114,11 +114,10 @@
         for n, (source, target) in enumerate(
             [
                 (h_hbm, h_ref),
-                (geo_hbm, geo_ref),
-                (tw_hbm, tw_ref),
-                (thi_hbm, thi_ref),
-                (tlo_hbm, tlo_ref),
-                (wt_hbm, wt_ref),
+                (fixed_hbm.at[pl.ds(576, 40)], geo_ref),
+                (fixed_hbm.at[pl.ds(512, 64)], tw_ref),
+                (fixed_hbm.at[pl.ds(0, 512)], table_ref),
+                (fixed_hbm.at[pl.ds(616, 64)], wt_ref),
                 (resp_hbm, resp_ref.at[pl.ds(0, SLOTS)]),
             ]
         )
@@ -205,15 +204,15 @@
         exchange_lon(send_a.at[side], recv_a.at[side], side)
 
     loads[1].wait()
-    x = geo_ref[0]
-    starts = pltpu.roll(geo_ref[4], lax.rem(DEV - me, DEV), axis=1)
+    x = geo_ref[0:8, :]
+    starts = pltpu.roll(geo_ref[32:40, :], lax.rem(DEV - me, DEV), axis=1)
     state = []
     for i in range(SLOTS):
         m = (DEV * i + me).astype(f32)
-        coarse = m * geo_ref[1]
-        fine = m * geo_ref[2] + jnp.broadcast_to(starts[i : i + 1, 0:1], (8, 128))
+        coarse = m * geo_ref[8:16, :]
+        fine = m * geo_ref[16:24, :] + jnp.broadcast_to(starts[i : i + 1, 0:1], (8, 128))
         count = jnp.maximum(jnp.ceil((-84.0 - (coarse + fine)) * (1.0 / 64.0)), 0.0)
-        value = jnp.exp2((coarse + 64.0 * count) + fine) * geo_ref[3]
+        value = jnp.exp2((coarse + 64.0 * count) + fine) * geo_ref[24:32, :]
         state.append((jnp.zeros_like(value), value, count))
 
     for section in range(SLOTS):
@@ -258,8 +257,8 @@
             real[rho], real[8 - rho] = a + b_, a - b_
             imag[rho], imag[8 - rho] = c + e, c - e
         for rho in range(LON):
-            tc = tw_ref[0, rho : rho + 1, lanes]
-            ts = tw_ref[1, rho : rho + 1, lanes]
+            tc = tw_ref[side * LON + rho : side * LON + rho + 1, :]
+            ts = tw_ref[(2 + side) * LON + rho : (2 + side) * LON + rho + 1, :]
             if rho % 8 == 0:
                 zre, zim = real[rho] * tc, -(real[rho] * ts)
             elif rho < 8:
@@ -271,10 +270,8 @@
             zs[rho, 0:ROWS, CELLS + side * 128 : CELLS + side * 128 + 128] = zim
 
     loads[3].wait()
-    loads[4].wait()
     zh, zl = split(zs[...].reshape(LON * 16, 2 * CELLS))
-    thi = thi_ref[...]
-    tlo = tlo_ref[...]
+    thi, tlo = split(table_ref[...])
     nn = (((1,), (0,)), ((), ()))
     nt = (((1,), (1,)), ((), ()))
 
@@ -321,8 +318,8 @@
 
     lax.fori_loop(0, TALL // 128, halves, 0)
 
+    loads[4].wait()
     loads[5].wait()
-    loads[6].wait()
     turned = pltpu.roll(resp_ref[...], lax.rem(DEV - me, DEV), axis=1)
     within = lax.broadcasted_iota(jnp.int32, (SLOTS, 128), 1) < DEV - me
     shifted = jnp.where(within, turned[0:SLOTS], turned[1 : SLOTS + 1])
@@ -396,8 +393,8 @@
         real = []
         imag = []
         for rho in range(LON):
-            tc = tw_ref[0, rho : rho + 1, lanes]
-            ts = tw_ref[1, rho : rho + 1, lanes]
+            tc = tw_ref[side * LON + rho : side * LON + rho + 1, :]
+            ts = tw_ref[(2 + side) * LON + rho : (2 + side) * LON + rho + 1, :]
             vre = vs[side, pl.ds(rho, ROWS, stride=16), :]
             vim = vs[2 + side, pl.ds(rho, ROWS, stride=16), :]
             real.append(vre * tc - vim * ts)
@@ -431,34 +428,28 @@
         for r in range(ROWS):
             recv_d[side, pl.ds(ROWS * lon + r, 1), :] = send_d[side, pl.ds(ROWS * lon + r, 1), :]
 
-    stores = []
     for side in range(2):
         lanes = slice(side * 128, side * 128 + 128)
         finish(send_d.at[side], recv_d.at[side], 4 + side, ROWS * (LON - 1))
-        store = pltpu.make_async_copy(recv_d.at[side], o_hbm.at[:, lanes], lsem.at[7 + side])
-        store.start()
-        stores.append(store)
-    for store in stores:
-        store.wait()
+        o_ref[:, lanes] = recv_d[side]
 
 
 def shards(height, response):
-    high, low, twiddle, geometry, weights = constants()
+    fixed = constants()
     hbm = pl.BlockSpec(memory_space=pltpu.HBM)
     blocks = pltpu.VMEM((2, LON, ROWS, 1, 128), f32)
     rows = pltpu.VMEM((DEV, 128), f32)
     out = pl.pallas_call(
         kernel,
         out_shape=jax.ShapeDtypeStruct((NLAT // LAT, CELLS), f32),
-        in_specs=[hbm] * 7,
-        out_specs=hbm,
+        in_specs=[hbm] * 3,
+        out_specs=pl.BlockSpec(memory_space=pltpu.VMEM),
         scratch_shapes=[
             pltpu.VMEM((NLAT // LAT, CELLS), f32),
             pltpu.VMEM((8, 128), f32),
-            pltpu.VMEM((2 * CELLS, 128), bf16),
-            pltpu.VMEM((2 * CELLS, 128), bf16),
-            pltpu.VMEM((2, LON, CELLS), f32),
-            pltpu.VMEM((5, 8, 128), f32),
+            pltpu.VMEM((2 * CELLS, 128), f32),
+            pltpu.VMEM((4 * LON, 128), f32),
+            pltpu.VMEM((40, 128), f32),
             pltpu.VMEM((HALF, 128), f32),
             blocks,
             blocks,
@@ -481,19 +472,15 @@
             pltpu.VMEM((2, NLAT // LAT, 128), f32),
             pltpu.SemaphoreType.DMA((6,)),
             pltpu.SemaphoreType.DMA((6,)),
-            pltpu.SemaphoreType.DMA((9,)),
+            pltpu.SemaphoreType.DMA((6,)),
         ],
         compiler_params=pltpu.CompilerParams(
-            collective_id=0, has_side_effects=True, vmem_limit_bytes=60 * 1024 * 1024
+            collective_id=0, has_side_effects=True, vmem_limit_bytes=40 * 1024 * 1024
         ),
     )(
-        height.reshape(NLAT // LAT, CELLS),
-        response.reshape(SLOTS, 128),
-        jnp.asarray(high),
-        jnp.asarray(low),
-        jnp.asarray(twiddle),
-        jnp.asarray(geometry),
-        jnp.asarray(weights),
+        pltpu.with_memory_space_constraint(height.reshape(NLAT // LAT, CELLS), pltpu.HBM),
+        pltpu.with_memory_space_constraint(response.reshape(SLOTS, 128), pltpu.HBM),
+        pltpu.with_memory_space_constraint(jnp.asarray(fixed), pltpu.HBM),
     )
     return out.reshape(height.shape)
 

time: 34.4 us -> 32.8 us (0.953)
  local copies, waits for them, and re-layouts: 1.58 us -> 0.66 us
  Pallas kernels: 32.7 us -> 32 us
    unnamed x1, local copies, waits for them, and re-layouts: 1.58 us -> 0.66 us
    pallas_call x1, Pallas kernels: 32.7 us -> 32 us  [shards(): pl.pallas_call(kernel, out_shape=jax.ShapeDtypeStruct((NLAT // LAT, CELLS...]
where the time goes in v5:
time: 32.8 us; the launch traced here: 32.7 us
  Pallas kernels  32 us (98%)
  local copies, waits for them, and re-layouts  0.66 us (2%)
    pallas_call x1, Pallas kernels, shards(): pl.pallas_call(kernel, out_shape=jax.ShapeDtypeStruct((NLAT // LAT, CELLS...  32 us
    unnamed x1, local copies, waits for them, and re-layouts  0.66 us

profile of v5, /device:TPU:1, one launch (start us, length us, event | category | flops | bytes accessed | tf_op | source)
XLA Modules:
  0.0 32.7 jit_solution(6627276396414822698)
XLA Ops:
  0.0 32.0 %shard_map.37 = f32[144,256]{1,0:T(8,128)S(1)} custom-call(f32[144,256]{1,0:T(8,128)} %bitcast.4, f32[5,128]{1,0:T(8,128)} %bitcast.5, f32[680,128]{1,0:T(8,128)} %constant.2.clone.fixed_hbm), custom_call_target="tpu_custom_call" | custom-call | tf_op jit(solution)/shard_map/pallas_call | solution.py:442
  32.0 0.7 %copy.5 = f32[1,144,256]{2,1,0:T(8,128)} copy(f32[1,144,256]{2,1,0:T(8,128)S(1)} %bitcast.3) | data formatting | bytes 294912

commit v6 on v5

--- a/solution.py
+++ b/solution.py
@@ -105,7 +105,7 @@
 
 def kernel(
     h_hbm, resp_hbm, fixed_hbm, o_ref,
-    h_ref, resp_ref, table_ref, tw_ref, geo_ref, wt_ref,
+    h_ref, resp_ref, table_ref, thi_ref, tlo_ref, tw_ref, geo_ref, wt_ref,
     send_a, recv_a, zs, osc, send_b, recv_b, coef_a, coef_c, tall, phi, plo, phi_t, plo_t, fold, send_c, recv_c, vs, send_d, recv_d,
     ssem, rsem, lsem,
 ):
@@ -122,9 +122,7 @@
             ]
         )
     ]
-    resp_ref[...] = jnp.zeros((8, 128), f32)
-    for load in loads:
-        load.start()
+    loads[0].start()
     lon = lax.axis_index("lon")
     lat = lax.axis_index("lat")
     me = lat * LON + lon
@@ -154,6 +152,9 @@
     for a, b in greeted:
         pl.semaphore_signal(barrier, inc=1, device_id={"lat": a, "lon": b})
 
+    resp_ref[...] = jnp.zeros((8, 128), f32)
+    for load in loads[1:]:
+        load.start()
     loads[0].wait()
 
     def stage(block, carry):
@@ -238,6 +239,8 @@
 
         state = list(lax.fori_loop(0, DEV // 8, steps, tuple(state[:active])))
 
+    loads[3].wait()
+    thi_ref[...], tlo_ref[...] = split(table_ref[...])
     loads[2].wait()
     for side in range(2):
         lanes = slice(side * 128, side * 128 + 128)
@@ -269,9 +272,8 @@
             zs[rho, 0:ROWS, lanes] = zre
             zs[rho, 0:ROWS, CELLS + side * 128 : CELLS + side * 128 + 128] = zim
 
-    loads[3].wait()
     zh, zl = split(zs[...].reshape(LON * 16, 2 * CELLS))
-    thi, tlo = split(table_ref[...])
+    thi, tlo = thi_ref[...], tlo_ref[...]
     nn = (((1,), (0,)), ((), ()))
     nt = (((1,), (1,)), ((), ()))
 
@@ -280,7 +282,7 @@
         both = lax.dot_general(jnp.concatenate([high, low], axis=0), other_high, dims, preferred_element_type=f32)
         return both[:count] + both[count:] + lax.dot_general(high, other_low, dims, preferred_element_type=f32)
 
-    osc[...] = product(zh, zl, thi, tlo, nn)
+    osc[0 : LON * 16, :] = product(zh, zl, thi, tlo, nn)
 
     lane = lax.broadcasted_iota(jnp.int32, (LON, 128), 1)
     packed = [jnp.zeros((LON, 128), f32) for _ in range(LAT)]
@@ -358,7 +360,8 @@
     pad = jnp.zeros((6, WIDE), f32)
     lhs = jnp.concatenate([jnp.concatenate(evens, axis=1), pad, jnp.concatenate(odds, axis=1), pad], axis=0)
     lh, ll = split(lhs)
-    sh, sl = split(product(lh, ll, phi_t[...], plo_t[...], nn) * gain)
+    used = ROWS * HALF
+    sh, sl = split(product(lh[:, :used], ll[:, :used], phi_t[:used], plo_t[:used], nn) * gain)
     synthesis = product(sh, sl, phi[...], plo[...], nn)
     fold[...] = jnp.zeros((128, 128), f32)
     for j in range(5):
@@ -386,7 +389,7 @@
     gh, gl = split(jnp.concatenate(gathered, axis=0))
     inverse = product(gh, gl, thi, tlo, nt)
     for c in range(4):
-        vs[c] = inverse[:, c * 128 : (c + 1) * 128]
+        vs[c, 0 : ROWS * LON, :] = inverse[:, c * 128 : (c + 1) * 128]
 
     for side in range(2):
         lanes = slice(side * 128, side * 128 + 128)
@@ -448,18 +451,20 @@
             pltpu.VMEM((NLAT // LAT, CELLS), f32),
             pltpu.VMEM((8, 128), f32),
             pltpu.VMEM((2 * CELLS, 128), f32),
+            pltpu.VMEM((2 * CELLS, 128), bf16),
+            pltpu.VMEM((2 * CELLS, 128), bf16),
             pltpu.VMEM((4 * LON, 128), f32),
             pltpu.VMEM((40, 128), f32),
             pltpu.VMEM((HALF, 128), f32),
             blocks,
             blocks,
             pltpu.VMEM((LON, 16, 2 * CELLS), f32),
-            pltpu.VMEM((LON * 16, 128), f32),
+            pltpu.VMEM((LON * 16 + 16, 128), f32),
             rows,
             rows,
             pltpu.VMEM((TALL, 128), f32),
             pltpu.VMEM((TALL, 128), f32),
-            pltpu.VMEM((TALL * 8, 128), f32),
+            pltpu.VMEM((TALL * 8 + 8, 128), f32),
             pltpu.VMEM((TALL, WIDE), bf16),
             pltpu.VMEM((TALL, WIDE), bf16),
             pltpu.VMEM((WIDE, TALL), bf16),
@@ -467,7 +472,7 @@
             pltpu.VMEM((128, 128), f32),
             rows,
             rows,
-            pltpu.VMEM((4, ROWS * LON, 128), f32),
+            pltpu.VMEM((4, 16 * LON + 16, 128), f32),
             pltpu.VMEM((2, NLAT // LAT, 128), f32),
             pltpu.VMEM((2, NLAT // LAT, 128), f32),
             pltpu.SemaphoreType.DMA((6,)),

time: 32.8 us -> 32.7 us (level)
  no operation moved by 1% of the time
where the time goes in v6:
time: 32.7 us; the launch traced here: 32.6 us
  Pallas kernels  31.9 us (98%)
  local copies, waits for them, and re-layouts  0.66 us (2%)
    pallas_call x1, Pallas kernels, shards(): pl.pallas_call(kernel, out_shape=jax.ShapeDtypeStruct((NLAT // LAT, CELLS...  31.9 us
    unnamed x1, local copies, waits for them, and re-layouts  0.66 us

profile of v6, /device:TPU:1, one launch (start us, length us, event | category | flops | bytes accessed | tf_op | source)
XLA Modules:
  0.0 32.6 jit_solution(2213913943210482650)
XLA Ops:
  0.0 31.9 %shard_map.37 = f32[144,256]{1,0:T(8,128)S(1)} custom-call(f32[144,256]{1,0:T(8,128)} %bitcast.4, f32[5,128]{1,0:T(8,128)} %bitcast.5, f32[680,128]{1,0:T(8,128)} %constant.2.clone.fixed_hbm), custom_call_target="tpu_custom_call" | custom-call | tf_op jit(solution)/shard_map/pallas_call | solution.py:445
  31.9 0.7 %copy.5 = f32[1,144,256]{2,1,0:T(8,128)} copy(f32[1,144,256]{2,1,0:T(8,128)S(1)} %bitcast.3) | data formatting | bytes 294912

commit v7 on v6

--- a/solution.py
+++ b/solution.py
@@ -161,8 +161,8 @@
         for r in range(ROWS):
             source = jnp.where(south == 1, ROWS - 1 - r, r)
             line = h_ref[pl.ds(ROWS * block + source, 1), :]
-            send_a[0, block, r] = line[:, :128]
-            send_a[1, block, r] = line[:, 128:]
+            send_a[block, 0, r] = line[:, :128]
+            send_a[block, 1, r] = line[:, 128:]
         return carry
 
     lax.fori_loop(0, LON, stage, 0)
@@ -201,8 +201,7 @@
         every.wait_send()
         every.wait_recv()
 
-    for side in range(2):
-        exchange_lon(send_a.at[side], recv_a.at[side], side)
+    exchange_lon(send_a, recv_a, 0)
 
     loads[1].wait()
     x = geo_ref[0:8, :]
@@ -244,8 +243,9 @@
     loads[2].wait()
     for side in range(2):
         lanes = slice(side * 128, side * 128 + 128)
-        finish(send_a.at[side], recv_a.at[side], side, LON - 1)
-        d = [recv_a[side, b, :, 0, :] for b in range(LON)]
+        if side == 0:
+            finish(send_a, recv_a, 0, LON - 1)
+        d = [recv_a[b, side, :, 0, :] for b in range(LON)]
         even = {b: d[b] + d[16 - b] for b in range(1, 8)}
         odd = {b: d[b] - d[16 - b] for b in range(1, 8)}
         real = [None] * 9
@@ -440,7 +440,7 @@
 def shards(height, response):
     fixed = constants()
     hbm = pl.BlockSpec(memory_space=pltpu.HBM)
-    blocks = pltpu.VMEM((2, LON, ROWS, 1, 128), f32)
+    blocks = pltpu.VMEM((LON, 2, ROWS, 1, 128), f32)
     rows = pltpu.VMEM((DEV, 128), f32)
     out = pl.pallas_call(
         kernel,

time: 32.7 us -> 32.8 us (level)
  no operation moved by 1% of the time
where the time goes in v7:
time: 32.8 us; the launch traced here: 32.7 us
  Pallas kernels  32 us (98%)
  local copies, waits for them, and re-layouts  0.66 us (2%)
    pallas_call x1, Pallas kernels, shards(): pl.pallas_call(kernel, out_shape=jax.ShapeDtypeStruct((NLAT // LAT, CELLS...  32 us
    unnamed x1, local copies, waits for them, and re-layouts  0.66 us

profile of v7, /device:TPU:1, one launch (start us, length us, event | category | flops | bytes accessed | tf_op | source)
XLA Modules:
  0.0 32.7 jit_solution(4027691632711742867)
XLA Ops:
  0.0 32.0 %shard_map.37 = f32[144,256]{1,0:T(8,128)S(1)} custom-call(f32[144,256]{1,0:T(8,128)} %bitcast.4, f32[5,128]{1,0:T(8,128)} %bitcast.5, f32[680,128]{1,0:T(8,128)} %constant.2.clone.fixed_hbm), custom_call_target="tpu_custom_call" | custom-call | tf_op jit(solution)/shard_map/pallas_call | solution.py:445
  32.0 0.7 %copy.5 = f32[1,144,256]{2,1,0:T(8,128)} copy(f32[1,144,256]{2,1,0:T(8,128)S(1)} %bitcast.3) | data formatting | bytes 294912

commit v8 on v6

--- a/solution.py
+++ b/solution.py
@@ -269,10 +269,11 @@
             else:
                 yre, yim = real[16 - rho], imag[16 - rho]
                 zre, zim = yre * tc - yim * ts, -(yim * tc) - yre * ts
-            zs[rho, 0:ROWS, lanes] = zre
-            zs[rho, 0:ROWS, CELLS + side * 128 : CELLS + side * 128 + 128] = zim
-
-    zh, zl = split(zs[...].reshape(LON * 16, 2 * CELLS))
+            mine = slice(rho * ROWS, rho * ROWS + ROWS)
+            zs[mine, lanes] = zre
+            zs[mine, CELLS + side * 128 : CELLS + side * 128 + 128] = zim
+
+    zh, zl = split(zs[...])
     thi, tlo = thi_ref[...], tlo_ref[...]
     nn = (((1,), (0,)), ((), ()))
     nt = (((1,), (1,)), ((), ()))
@@ -282,12 +283,12 @@
         both = lax.dot_general(jnp.concatenate([high, low], axis=0), other_high, dims, preferred_element_type=f32)
         return both[:count] + both[count:] + lax.dot_general(high, other_low, dims, preferred_element_type=f32)
 
-    osc[0 : LON * 16, :] = product(zh, zl, thi, tlo, nn)
+    osc[0 : LON * ROWS, :] = product(zh, zl, thi, tlo, nn)
 
     lane = lax.broadcasted_iota(jnp.int32, (LON, 128), 1)
     packed = [jnp.zeros((LON, 128), f32) for _ in range(LAT)]
     for r in range(ROWS):
-        value = osc[pl.ds(r, LON, stride=16), :]
+        value = osc[pl.ds(r, LON, stride=ROWS), :]
         mine = jnp.logical_and(lane >= 10 * r, lane < 10 * r + 10)
         for g in range(LAT):
             shift = (10 * (r - g)) % 128
@@ -458,8 +459,8 @@
             pltpu.VMEM((HALF, 128), f32),
             blocks,
             blocks,
-            pltpu.VMEM((LON, 16, 2 * CELLS), f32),
-            pltpu.VMEM((LON * 16 + 16, 128), f32),
+            pltpu.VMEM((LON * ROWS, 2 * CELLS), f32),
+            pltpu.VMEM((LON * ROWS + 16, 128), f32),
             rows,
             rows,
             pltpu.VMEM((TALL, 128), f32),

time: 32.7 us -> 32.6 us (level)
  no operation moved by 1% of the time
where the time goes in v8:
time: 32.6 us; the launch traced here: 32.5 us
  Pallas kernels  31.8 us (98%)
  local copies, waits for them, and re-layouts  0.66 us (2%)
    pallas_call x1, Pallas kernels, shards(): pl.pallas_call(kernel, out_shape=jax.ShapeDtypeStruct((NLAT // LAT, CELLS...  31.8 us
    unnamed x1, local copies, waits for them, and re-layouts  0.66 us

profile of v8, /device:TPU:1, one launch (start us, length us, event | category | flops | bytes accessed | tf_op | source)
XLA Modules:
  0.0 32.5 jit_solution(16860541756899722699)
XLA Ops:
  0.0 31.8 %shard_map.37 = f32[144,256]{1,0:T(8,128)S(1)} custom-call(f32[144,256]{1,0:T(8,128)} %bitcast.4, f32[5,128]{1,0:T(8,128)} %bitcast.5, f32[680,128]{1,0:T(8,128)} %constant.2.clone.fixed_hbm), custom_call_target="tpu_custom_call" | custom-call | tf_op jit(solution)/shard_map/pallas_call | solution.py:446
  31.8 0.7 %copy.5 = f32[1,144,256]{2,1,0:T(8,128)} copy(f32[1,144,256]{2,1,0:T(8,128)S(1)} %bitcast.3) | data formatting | bytes 294912
